TPU v7x, 128 devices: a whole 4x4x4 slice. The times are simulated.
128 devices in a mesh: dp: 32 (over x, y, core), group: 4 (over z).
Axes of the slice: x: 4, y: 4, z: 4, core: 2. Of those that a mesh axis runs over, the one named last changes fastest.
Arguments:
- images: bfloat16 [16384, 512], P(('dp', 'group')), may hold values from -1 to 1
- texts: bfloat16 [16384, 512], P(('dp', 'group')), may hold values from -1 to 1
- log_scale: float32 [], replicated, may hold values from 2 to 2.7
Outputs:
- grad_images: bfloat16 [16384, 512], P(('dp', 'group'))
- grad_texts: bfloat16 [16384, 512], P(('dp', 'group'))
- loss: float32 [], replicated
- grad_scale: float32 [], replicated
All inputs are finite; a program needn't handle non-finite values.
Results may differ from a plain program's by a relative error of at most 0.0013.
The roundings to bfloat16 on the way count: a program that leaves them out, or rounds other values in their place, can miss the bound.
Values may be sent and summed in bfloat16 or wider, within the bound.
A program may use at most 128 MiB of HBM per device.

v0:
```python
import jax
import jax.numpy as jnp
from jax import lax
from jax.sharding import Mesh
from jax.sharding import PartitionSpec as P

DP_GROUP = ("dp_0", "dp_1", "dp_2", "group")


def in_one_piece(arrays, axis, split_dim, concat_dim, along):
    ends, at = ([], 0)
    for a in arrays[:-1]:
        at += a.shape[along]
        ends.append(at)
    both = jnp.concatenate(arrays, axis=along)
    return tuple(
        jnp.split(
            lax.all_to_all(both, axis, split_axis=split_dim, concat_axis=concat_dim, tiled=True),
            ends,
            axis=along,
        )
    )


def rows_first(arrays, axis, dims):
    turned = [jnp.moveaxis(a, dim, 0) for a, dim in zip(arrays, dims)]
    both = jnp.concatenate([t.reshape(len(t), -1) for t in turned], axis=1)
    filled, at, outs = (lax.all_gather(both, axis, axis=0, tiled=True), 0, [])
    for t, dim in zip(turned, dims):
        share = filled[:, at : at + t[0].size].reshape(-1, *t.shape[1:])
        outs.append(jnp.moveaxis(share, 0, dim))
        at += t[0].size
    return tuple(outs)


def one_axis_at_a_time(value, axes):
    for axis in axes:
        value = lax.psum(value, axis)
    return value


def body(images, texts, log_scale):
    row_count = images.shape[0]
    device_count = lax.axis_size(DP_GROUP)
    pair_total = row_count * device_count
    texts_whole = lax.all_gather(texts, DP_GROUP, axis=0, tiled=True)
    images_whole = lax.all_gather(images, DP_GROUP, axis=0, tiled=True)
    logit_scale = jnp.exp(log_scale)
    first_pair = lax.axis_index(DP_GROUP) * row_count
    contract_last = (((1,), (1,)), ((), ()))
    contract_first = (((0,), (0,)), ((), ()))
    row_logits = logit_scale * lax.dot_general(
        images, texts_whole, contract_last, preferred_element_type=jnp.float32
    )
    row_top = jnp.max(row_logits, axis=1)
    row_lse = row_top + jnp.log(jnp.sum(jnp.exp(row_logits - row_top[:, None]), axis=1))
    paired = jnp.diagonal(lax.dynamic_slice_in_dim(row_logits, first_pair, row_count, 1))
    part_top = jnp.max(row_logits, axis=0)
    part_sum = jnp.sum(jnp.exp(row_logits - part_top[None, :]), axis=0)
    got_top, got_sum = in_one_piece(
        (part_top.reshape(device_count, row_count), part_sum.reshape(device_count, row_count)),
        DP_GROUP,
        0,
        0,
        1,
    )
    col_top = jnp.max(got_top, axis=0)
    col_lse = col_top + jnp.log(jnp.sum(got_sum * jnp.exp(got_top - col_top[None, :]), axis=0))
    row_whole, col_whole = rows_first((row_lse, col_lse), DP_GROUP, (0, 0))
    own_pairs = (
        jnp.arange(pair_total)[None, :] == (first_pair + jnp.arange(row_count))[:, None]
    ).astype(jnp.float32)
    row_grad = (
        0.5 * (jnp.exp(row_logits - row_lse[:, None]) + jnp.exp(row_logits - col_whole[None, :]))
        - own_pairs
    )
    scale_part = jnp.sum(row_grad * row_logits)
    row_weights = row_grad.astype(jnp.bfloat16)
    grad_images = (
        logit_scale * jnp.dot(row_weights, texts_whole, preferred_element_type=jnp.float32)
    ).astype(jnp.bfloat16)
    col_logits = logit_scale * lax.dot_general(
        images_whole, texts, contract_last, preferred_element_type=jnp.float32
    )
    col_grad = (
        0.5 * (jnp.exp(col_logits - row_whole[:, None]) + jnp.exp(col_logits - col_lse[None, :]))
        - own_pairs.T
    )
    text_sum = logit_scale * lax.dot_general(
        col_grad.astype(jnp.bfloat16),
        images_whole,
        contract_first,
        preferred_element_type=jnp.float32,
    )
    grad_texts = text_sum.astype(jnp.bfloat16)
    loss_part = jnp.sum(row_lse) + jnp.sum(col_lse) - 2.0 * jnp.sum(paired)
    loss_total, scale_total = (
        one_axis_at_a_time(loss_part, DP_GROUP),
        one_axis_at_a_time(scale_part, DP_GROUP),
    )
    return (grad_images, grad_texts, loss_total / (2.0 * pair_total), scale_total / pair_total)


def solution(mesh):
    split = Mesh(
        mesh.devices.reshape(4, 4, 2, mesh.shape["group"]), ("dp_0", "dp_1", "dp_2", "group")
    )
    placed = (P(DP_GROUP, None), P(DP_GROUP, None), P())
    return jax.shard_map(
        body,
        mesh=split,
        in_specs=placed,
        out_specs=(P(DP_GROUP, None), P(DP_GROUP, None), P(), P()),
        check_vma=False,
    )
```

profile of v0, /device:TPU:1, one launch (start us, length us, event | category | flops | bytes accessed | tf_op | source)
XLA Modules:
  0.0 262.8 jit_solution(17786985613269034500)
XLA Ops:
  7.2 0.0 all-gather.3.cloned.1.call-start
  7.2 0.7 all-gather.3.cloned.1.call-update
  7.9 0.0 all-gather.5.cloned.1.call-start
  7.9 0.7 all-gather.5.cloned.1.call-update
  9.4 85.4 %all-gather.3.cloned.1.call-done = bf16[16384,512]{1,0:T(8,128)(2,1)} async-done(((bf16[128,512]{1,0:T(8,128)(2,1)}), bf16[16384,512]{1,0:T(8,128)(2,1)}) %all-gather.3.cloned.1.call-update) | async-done | bytes 16777232 | tf_op jit(solution)/shard_map/all_gather | solution.py:46
  94.7 14.5 %fusion.19 = (f32[128]{0:T(128)S(1)}, f32[16384]{0:T(1024)S(1)}, f32[128,16384]{1,0:T(8,128)}) fusion(bf16[128,512]{1,0:T(8,128)(2,1)} %param.3, bf16[16384,512]{1,0:T(8,128)(2,1)} %all-gather.3.cloned.1.call-done, f32[]{:T(128)S(6)} %exp.24), kind=kOutput, calls=%fused_computation.34 | convolution fusion | flops 2153758720 | bytes 25362948 | tf_op jit(solution)/shard_map/dot_general | solution.py:52
  109.2 4.7 %exponential_reduce_fusion.1 = (f32[128]{0:T(128)S(1)}, f32[16384]{0:T(1024)S(1)}) fusion(f32[128,16384]{1,0:T(8,128)} %get-tuple-element.22, f32[128]{0:T(128)S(1)} %get-tuple-element.6, f32[16384]{0:T(1024)S(1)} %get-tuple-element.7), kind=kLoop, calls=%fused_computation.9 | loop fusion | flops 8372096 | bytes 8520704 | tf_op jit(solution)/shard_map/reduce_sum | solution.py:56
  114.0 0.7 all_to_all.8
  114.7 7.4 %all-to-all-start = ((f32[128,1,256]{2,1,0:T(1,128)}), f32[128,1,256]{2,1,0:T(1,128)S(1)}, u32[]{:S(2)}, u32[]{:S(2)}) async-start(f32[128,1,256]{2,1,0:T(1,128)} %all_to_all.8), calls=%async_computation | async-start | bytes 262144 | tf_op jit(solution)/shard_map/all_to_all | solution.py:18
  122.2 0.9 constant_dynamic-slice_fusion
  123.0 1.2 gather_fusion
  124.3 0.6 reduce_sum.68
  125.5 0.6 fusion.21
  126.1 5.9 %all-to-all-done = f32[128,1,256]{2,1,0:T(1,128)S(1)} async-done(((f32[128,1,256]{2,1,0:T(1,128)}), f32[128,1,256]{2,1,0:T(1,128)S(1)}, u32[]{:S(2)}, u32[]{:S(2)}) %all-to-all-start) | async-done | bytes 131104 | tf_op jit(solution)/shard_map/all_to_all | solution.py:18
  132.1 0.6 fusion.20
  134.0 50.9 %all_gather.10 = f32[16384,2]{0,1:T(2,128)S(1)} all-gather(f32[128,2]{0,1:T(2,128)S(1)} %pad_maximum_fusion.1), channel_id=1, replica_groups=mesh['dp_0'=4,'dp_1'=4,'dp_2'=2,'group'=4] {'dp_0','dp_1','dp_2','group'}, dimensions={0}, use_global_device_ids=true | all-gather | bytes 132096 | tf_op jit(solution)/shard_map/all_gather | solution.py:28
  185.0 0.1 fusion.22
  185.1 6.5 %multiply_reduce_fusion = f32[]{:T(128)} fusion(f32[128,16384]{1,0:T(8,128)} %get-tuple-element.22, s32[128]{0:T(128)S(1)} %iota_add_fusion, f32[16384]{0:T(1024)S(1)} %bitcast.20, f32[128]{0:T(128)S(1)} %get-tuple-element.19), kind=kLoop, calls=%fused_computation.3 | loop fusion | flops 18874368 | bytes 8455172 | tf_op jit(solution)/shard_map/reduce_sum | solution.py:77
  191.6 8.4 %all-reduce.2 = (f32[]{:T(128)}, f32[]{:T(128)}) all-reduce(f32[]{:T(128)S(6)} %sub.87, f32[]{:T(128)} %multiply_reduce_fusion), channel_id=1, replica_groups=mesh['dp_0'=4,'dp_1'=4,'dp_2'=2,'group'=4] {'dp_0'}, use_global_device_ids=true, to_apply=%region_9.10 | all-reduce | flops 2 | bytes 16 | tf_op jit(solution)/shard_map/psum | solution.py:38
  200.0 9.5 %all-reduce.1 = (f32[]{:T(128)}, f32[]{:T(128)}) all-reduce(f32[]{:T(128)} %get-tuple-element.12, f32[]{:T(128)} %get-tuple-element.13), channel_id=1, replica_groups=mesh['dp_0'=4,'dp_1'=4,'dp_2'=2,'group'=4] {'dp_1'}, use_global_device_ids=true, to_apply=%region_10.11 | all-reduce | flops 2 | bytes 16 | tf_op jit(solution)/shard_map/psum | solution.py:38
  209.5 4.0 %all-reduce.3 = (f32[]{:T(128)}, f32[]{:T(128)}) all-reduce(f32[]{:T(128)} %get-tuple-element.10, f32[]{:T(128)} %get-tuple-element.11), channel_id=1, replica_groups=mesh['dp_0'=4,'dp_1'=4,'dp_2'=2,'group'=4] {'dp_2'}, use_global_device_ids=true, to_apply=%region_11.12 | all-reduce | flops 2 | bytes 16 | tf_op jit(solution)/shard_map/psum | solution.py:38
  213.5 8.0 %all-reduce = (f32[]{:T(128)}, f32[]{:T(128)}) all-reduce(f32[]{:T(128)} %get-tuple-element.14, f32[]{:T(128)} %get-tuple-element.15), channel_id=1, replica_groups=mesh['dp_0'=4,'dp_1'=4,'dp_2'=2,'group'=4] {'group'}, use_global_device_ids=true, to_apply=%region_12.13 | all-reduce | flops 2 | bytes 16 | tf_op jit(solution)/shard_map/psum | solution.py:38
  222.8 0.0 copy-start
  222.8 12.4 %fusion.12 = bf16[128,512]{1,0:T(8,128)(2,1)} fusion(bf16[16384,512]{1,0:T(8,128)(2,1)} %all-gather.3.cloned.1.call-done, f32[128,16384]{1,0:T(8,128)} %get-tuple-element.22, s32[128]{0:T(128)S(1)} %iota_add_fusion, f32[16384]{0:T(1024)S(1)} %bitcast.21, f32[128]{0:T(128)S(1)} %get-tuple-element.19, f32[]{:T(128)S(6)} %exp.24), kind=kOutput, calls=%fused_computation.19 | convolution fusion | flops 2164391936 | bytes 25363460 | tf_op jit(solution)/shard_map/dot_general | solution.py:80
  235.2 0.0 all-gather.5.cloned.1.call-done
  235.2 0.0 copy-done
  235.2 18.5 %fusion.15 = bf16[128,512]{1,0:T(8,128)(2,1)} fusion(bf16[16384,512]{1,0:T(8,128)(2,1)} %all-gather.5.cloned.1.call-done, bf16[128,512]{1,0:T(8,128)(2,1)S(1)} %copy-done, s32[128]{0:T(128)S(1)} %iota_add_fusion, f32[128]{0:T(128)S(1)} %get-tuple-element.17, f32[16384]{0:T(1024)S(1)} %bitcast.23, f32[]{:T(128)S(6)} %exp.24), kind=kOutput, calls=%fused_computation.20 | convolution fusion | flops 4313972736 | bytes 17105924 | tf_op jit(solution)/shard_map/dot_general | solution.py:89
  (7 shorter events, 0.1 us)
Async XLA Ops:
  7.2 87.6 %all-gather.3.cloned.1.call-start = ((), (), s32[]{:S(2)}) async-start(), calls=%async_computation.1 | async-start | bytes 16908288 | tf_op jit(solution)/shard_map/all_gather | solution.py:46
  7.9 227.3 %all-gather.5.cloned.1.call-start = ((), (), s32[]{:S(2)}) async-start(), calls=%async_computation.2 | async-start | bytes 16908288 | tf_op jit(solution)/shard_map/all_gather | solution.py:47
  114.7 17.3 %all-to-all-start = ((f32[128,1,256]{2,1,0:T(1,128)}), f32[128,1,256]{2,1,0:T(1,128)S(1)}, u32[]{:S(2)}, u32[]{:S(2)}) async-start(f32[128,1,256]{2,1,0:T(1,128)} %all_to_all.8), calls=%async_computation | async-start | bytes 262144 | tf_op jit(solution)/shard_map/all_to_all | solution.py:18
  222.8 12.4 %copy-start = (bf16[128,512]{1,0:T(8,128)(2,1)S(1)}, bf16[128,512]{1,0:T(8,128)(2,1)}, u32[]{:S(2)}) copy-start(bf16[128,512]{1,0:T(8,128)(2,1)} %param.4) | copy-start | bytes 393220
Sparse Core Ops, SparseCore 0:
  11.1 83.5 all-gather.2
  97.9 79.5 all-gather.4
where the time goes:
time: 264 us; the launch traced here: 263 us
  waiting for transfers between devices  92.6 us (35%)
  blocking collectives  80.8 us (31%)
  matrix products  45.4 us (17%)
  between operations  20.3 us (8%)
  other arithmetic  13.2 us (5%)
  starting transfers between devices  7.49 us (3%)
  local copies, waits for them, and re-layouts  2.96 us (1%)
    all_gather x1, waiting for transfers between devices, body(): texts_whole = lax.all_gather(texts, DP_GROUP, axis=0, tiled=True)  85.4 us
    all_gather x1, blocking collectives, rows_first(): filled, at, outs = (lax.all_gather(both, axis, axis=0, tiled=True), 0, [])  50.9 us
    psum x4, blocking collectives, one_axis_at_a_time(): value = lax.psum(value, axis)  29.9 us
    dot_general x1, matrix products, body(): lax.dot_general(col_grad.astype(jnp.bfloat16), images_whole, contract_fir...  18.5 us
    dot_general x1, matrix products, body(): lax.dot_general(images, texts_whole, contract_last, preferred_element_typ...  14.5 us
    dot_general x1, matrix products, body(): jnp.dot(row_weights, texts_whole, preferred_element_type=jnp.float32)  12.4 us
    all_to_all x1, starting transfers between devices, in_one_piece(): lax.all_to_all(both, axis, split_axis=split_dim, concat_axis=concat_dim,...  7.42 us
    reduce_sum x1, other arithmetic, body(): scale_part = jnp.sum(row_grad * row_logits)  6.49 us
  transfers between devices with their start and end apart: 3, of which 2 were waited for; matrix products, arithmetic and copies ran while one was open for 16% of the time, Pallas kernels for 0%

commit v1 on v0

v1 whole, which is shorter than its diff:
```python
import functools
import math

import jax
import jax.numpy as jnp
from jax import lax
from jax.experimental import pallas as pl
from jax.experimental.pallas import tpu as pltpu
from jax.sharding import Mesh
from jax.sharding import PartitionSpec as P

AXES = ("x", "y", "core", "z")
CUBE = ("x", "y", "z")
MESH = pl.DeviceIdType.MESH
ROWS = 128
LOG2E = math.log2(math.e)
LN2 = math.log(2.0)
NT = (((1,), (1,)), ((), ()))


def kernel(
    dims, total,
    log_scale, images, texts,
    gi_out, gt_out, stats_out,
    X, XT, T, L, W, RM, RS, CM, CS, RL, CL, RREP, CROW,
    PI, RI, PT, RTC, RT, ST,
    local_sem, xs, xr, ts, tr, ds, dr, rls, rlr, cls, clr, pis, pir, pcs, pcr, pts, ptr, sts, str_,
):
    nd = len(dims)
    nb = 2**nd
    rows = nb * ROWS
    me = {a: lax.axis_index(a) for a in AXES}
    core = me["core"]

    def peer(mask, kind, flip):
        ident = {}
        for d, a in enumerate(dims):
            if mask >> d & 1:
                c = me[a]
                ident[a] = c + 1 - 2 * (c % 2) if kind == "A" else 3 - c
        if flip:
            ident["core"] = 1 - core
        return ident

    def spot(mask, kind):
        at = 0
        for d, a in enumerate(dims):
            bit = me[a] % 2 if kind == "A" else me[a] // 2
            at = at + 2**d * (1 - bit if mask >> d & 1 else bit)
        return at

    def send(src, dst, s, r, where):
        return pltpu.make_async_remote_copy(
            src_ref=src, dst_ref=dst, send_sem=s, recv_sem=r, device_id=where, device_id_type=MESH
        )

    def block(ref, m, n=ROWS):
        return ref.at[pl.ds(m * n, n)]

    ci = pltpu.make_async_copy(images, block(X, 0), local_sem.at[0])
    ct = pltpu.make_async_copy(texts, block(T, 0), local_sem.at[1])
    ci.start()
    ct.start()
    barrier = pltpu.get_barrier_semaphore()
    others = [(m, "A", False) for m in range(1, nb)]
    others += [(m, "B", f) for m in range(nb) for f in (False, True) if m or f]
    for o in others:
        pl.semaphore_signal(barrier, inc=1, device_id=peer(*o), device_id_type=MESH)
    ci.wait()
    ct.wait()
    pl.semaphore_wait(barrier, len(others))

    xc = [send(block(X, 0), block(X, m), xs.at[m], xr.at[m], peer(m, "A", False)) for m in range(1, nb)]
    tc = [send(block(T, 0), block(T, 2 * m), ts.at[m], tr.at[m], peer(m, "B", False)) for m in range(1, nb)]
    dc = [send(block(T, 2 * m), block(T, 2 * m + 1), ds.at[m], dr.at[m], peer(0, "B", True)) for m in range(nb)]
    dc[0].start()
    for a, b in zip(xc, tc):
        a.start()
        b.start()
    for m in range(1, nb):
        tc[m - 1].wait_recv()
        dc[m].start()
    for c in xc:
        c.wait_recv()
    for c in dc:
        c.wait_recv()
    for c in xc + tc + dc:
        c.wait_send()

    scale = jnp.exp(jnp.full((1, 128), log_scale[0], jnp.float32))
    scale_two = jnp.concatenate([scale * LOG2E] * 2, axis=1)
    XT[...] = X[...].T

    RM[...] = jnp.full(RM.shape, -3e38, jnp.float32)

    def logits(m, _):
        cols = pl.ds(pl.multiple_of(m * 256, 256), 256)
        v = lax.dot_general(X[...], T[cols, :], NT, preferred_element_type=jnp.float32) * scale_two
        L[:, cols] = v
        RM[...] = jnp.maximum(RM[...], jnp.maximum(v[:, :128], v[:, 128:]))
        CM[:, cols] = jnp.max(v, axis=0, keepdims=True)
        return 0

    lax.fori_loop(0, nb, logits, 0)

    def spread(m, _):
        at = pl.ds(pl.multiple_of(m * 128, 128), 128)
        RM[at, :] = jnp.broadcast_to(jnp.max(RM[at, :], axis=1, keepdims=True), (128, 128))
        return 0

    lax.fori_loop(0, nb, spread, 0)
    RS[...] = jnp.zeros(RS.shape, jnp.float32)

    def sums(m, _):
        cols = pl.ds(pl.multiple_of(m * 256, 256), 256)
        cm = CM[:, cols]

        def strip(i, cs):
            at = pl.ds(pl.multiple_of(i * 64, 64), 64)
            v = L[at, cols]
            rm = RM[at, :]
            er0 = jnp.exp2(v[:, :128] - rm)
            er1 = jnp.exp2(v[:, 128:] - rm)
            RS[at, :] = RS[at, :] + (er0 + er1)
            ec = jnp.exp2(v - cm)
            return cs + jnp.sum(ec.reshape(8, 8, 256), axis=0)

        cs = lax.fori_loop(0, rows // 64, strip, jnp.zeros((8, 256), jnp.float32))
        CS[:, cols] = jnp.sum(cs, axis=0, keepdims=True)
        return 0

    lax.fori_loop(0, nb, sums, 0)

    for m in range(nb):
        at = slice(m * 128, (m + 1) * 128)
        top = jnp.max(RM[at, :].T, axis=0, keepdims=True)
        part = jnp.sum(RS[at, :].T, axis=0, keepdims=True)
        RL[0, pl.ds(spot(m, "A"), 1), :] = top + jnp.log2(part)
    ccol = CM[...] + jnp.log2(CS[...])
    for m in range(nb):
        for f in range(2):
            at = (2 * m + f) * 128
            line = (1 - core if f else core) * nb + spot(m, "B")
            CL[0, pl.ds(line, 1), :] = ccol[:, at : at + 128]
    rc = [send(RL.at[0], RL.at[m], rls.at[m], rlr.at[m], peer(m, "A", False)) for m in range(1, nb)]
    cc = [
        send(CL.at[0], CL.at[2 * m + f], cls.at[2 * m + f], clr.at[2 * m + f], peer(m, "B", f == 1))
        for m in range(nb) for f in range(2) if m or f
    ]
    for c in cc + rc:
        c.start()
    for c in cc + rc:
        c.wait_recv()
    for c in cc + rc:
        c.wait_send()

    def joined(parts):
        top = functools.reduce(jnp.maximum, parts)
        return top + jnp.log2(functools.reduce(jnp.add, [jnp.exp2(p - top) for p in parts]))

    row_all = joined([RL[m] for m in range(nb)])
    col_all = joined([CL[m] for m in range(2 * nb)])
    RL[0] = row_all
    CL[0] = col_all
    for m in range(nb):
        line = RL[0, pl.ds(spot(m, "A"), 1), :]
        RREP[m * 128 : (m + 1) * 128, :] = jnp.broadcast_to(line + 1.0, (128, 128)).T
        for f in range(2):
            at = (2 * m + f) * 128
            CROW[:, at : at + 128] = CL[0, pl.ds((1 - core if f else core) * nb + spot(m, "B"), 1), :] + 1.0

    eye = (lax.broadcasted_iota(jnp.int32, (128, 128), 0) == lax.broadcasted_iota(jnp.int32, (128, 128), 1))
    own = L[:128, :128]
    paired = jnp.sum(jnp.where(eye, own, 0.0))
    loss_part = LN2 * (
        jnp.sum(RL[0, pl.ds(spot(0, "A"), 1), :]) + jnp.sum(CL[0, pl.ds(core * nb + spot(0, "B"), 1), :]) - 2.0 * paired
    )

    def weigh(m, acc):
        cols = pl.ds(pl.multiple_of(m * 256, 256), 256)
        cl = CROW[:, cols]

        def strip(i, acc):
            at = pl.ds(pl.multiple_of(i * 64, 64), 64)
            v = L[at, cols]
            rl = RREP[at, :]
            rl = jnp.concatenate([rl, rl], axis=1)
            w = jnp.exp2(v - rl) + jnp.exp2(v - cl)
            W[at, cols] = w.astype(jnp.bfloat16)
            return acc + jnp.sum((w * v).reshape(8, 8, 256), axis=0)

        return lax.fori_loop(0, rows // 64, strip, acc)

    acc = lax.fori_loop(0, nb, weigh, jnp.zeros((8, 256), jnp.float32))
    w = jnp.exp2(own - RREP[:128, :]) + jnp.exp2(own - CROW[:, :128])
    W[:128, :128] = (w - eye.astype(jnp.float32)).astype(jnp.bfloat16)
    scale_part = LN2 * (jnp.sum(acc) - paired)

    def image_grad(i, _):
        at = pl.ds(pl.multiple_of(i * 256, 256), 256)
        PI[at, :] = jnp.dot(W[at, :], T[...], preferred_element_type=jnp.float32)
        return 0

    lax.fori_loop(0, rows // 256, image_grad, 0)
    ic = [send(block(PI, m), block(RI, m), pis.at[m], pir.at[m], peer(m, "A", False)) for m in range(1, nb)]
    for c in ic:
        c.start()

    def text_grad(m, _):
        cols = pl.ds(pl.multiple_of(m * 256, 256), 256)
        v = jnp.dot(XT[...], W[:, cols], preferred_element_type=jnp.float32)
        PT[0, m] = v[:, :128]
        PT[1, m] = v[:, 128:]
        return 0

    lax.fori_loop(0, nb, text_grad, 0)
    pc = [send(PT.at[1, m], RTC.at[m], pcs.at[m], pcr.at[m], peer(0, "B", True)) for m in range(nb)]
    oc = [send(PT.at[0, m], RT.at[m], pts.at[m], ptr.at[m], peer(m, "B", False)) for m in range(1, nb)]
    for m in reversed(range(nb)):
        pc[m].start()
    for m in reversed(range(nb)):
        pc[m].wait_recv()
        PT[0, m] = PT[0, m] + RTC[m]
        if m:
            oc[m - 1].start()

    line = lax.broadcasted_iota(jnp.int32, (8, 128), 0)
    tile = jnp.where(line == 0, loss_part, jnp.where(line == 1, scale_part, 0.0))
    base = 0
    for kind, masks, flip in (("A", range(1, nb), False), ("B", range(1, nb), False), ("B", (0,), True)):
        ST[base] = tile
        copies = [
            send(ST.at[base], ST.at[base + 1 + i], sts.at[base + i], str_.at[base + i], peer(m, kind, flip))
            for i, m in enumerate(masks)
        ]
        for c in copies:
            c.start()
        for c in copies:
            c.wait_recv()
        for i in range(len(copies)):
            tile = tile + ST[base + 1 + i]
        for c in copies:
            c.wait_send()
        base += 1 + len(copies)
    stats_out[...] = jnp.where(line == 0, tile * (0.5 / total), tile * (1.0 / total))

    for c in ic:
        c.wait_recv()
    gi = PI[:128, :]
    for m in range(1, nb):
        gi = gi + RI[m * 128 : (m + 1) * 128, :]
    gi_out[...] = (gi * scale[:, :1]).astype(jnp.bfloat16)
    for c in oc:
        c.wait_recv()
    gt = PT[0, 0]
    for m in range(1, nb):
        gt = gt + RT[m]
    gt_out[...] = (gt * scale).T.astype(jnp.bfloat16)
    for c in ic + pc + oc:
        c.wait_send()


def body(dims, total, images, texts, log_scale):
    nb = 2 ** len(dims)
    f32, bf16 = jnp.float32, jnp.bfloat16
    vm, dma = pltpu.VMEM, pltpu.SemaphoreType.DMA
    width = images.shape[1]
    rows, cols = nb * ROWS, 2 * nb * ROWS
    gi, gt, stats = pl.pallas_call(
        functools.partial(kernel, dims, total),
        out_shape=(
            jax.ShapeDtypeStruct(images.shape, bf16),
            jax.ShapeDtypeStruct(texts.shape, bf16),
            jax.ShapeDtypeStruct((8, 128), f32),
        ),
        in_specs=[
            pl.BlockSpec(memory_space=pltpu.SMEM),
            pl.BlockSpec(memory_space=pl.ANY),
            pl.BlockSpec(memory_space=pl.ANY),
        ],
        out_specs=(pl.BlockSpec(memory_space=vm),) * 3,
        scratch_shapes=[
            vm((rows, width), bf16), vm((width, rows), bf16), vm((cols, width), bf16),
            vm((rows, cols), f32), vm((rows, cols), bf16),
            vm((rows, 128), f32), vm((rows, 128), f32), vm((1, cols), f32), vm((1, cols), f32),
            vm((nb, nb, 128), f32), vm((2 * nb, 2 * nb, 128), f32), vm((rows, 128), f32), vm((1, cols), f32),
            vm((rows, width), f32), vm((rows, width), f32),
            vm((2, nb, width, 128), f32), vm((nb, width, 128), f32), vm((nb, width, 128), f32),
            vm((2 * nb + 2, 8, 128), f32),
            dma((2,)), dma((nb,)), dma((nb,)), dma((nb,)), dma((nb,)), dma((nb,)), dma((nb,)),
            dma((nb,)), dma((nb,)), dma((2 * nb,)), dma((2 * nb,)),
            dma((nb,)), dma((nb,)), dma((nb,)), dma((nb,)), dma((nb,)), dma((nb,)),
            dma((2 * nb + 2,)), dma((2 * nb + 2,)),
        ],
        compiler_params=pltpu.CompilerParams(
            collective_id=0, has_side_effects=True, vmem_limit_bytes=60 * 2**20
        ),
        name="contrastive",
    )(log_scale.reshape(1), images, texts)
    return gi, gt, stats[0, 0], stats[1, 0]


def solution(mesh):
    return build(Mesh(mesh.devices.reshape(4, 4, 2, 4), AXES))


def build(split):
    dims = tuple(a for a in CUBE if split.shape[a] == 4)
    placed = P(AXES, None)
    return jax.shard_map(
        functools.partial(body, dims, ROWS * split.size),
        mesh=split,
        in_specs=(placed, placed, P()),
        out_specs=(placed, placed, P(), P()),
        check_vma=False,
    )
```

time: 264 us -> 93.6 us (0.35)
  waiting for transfers between devices: 92.6 us -> 0 us
  Pallas kernels: 0 us -> 88.6 us
  blocking collectives: 80.8 us -> 0 us
  matrix products: 45.4 us -> 0 us
  between operations: 20.3 us -> 1.29 us
  other arithmetic: 13.2 us -> 0 us
  starting transfers between devices: 7.49 us -> 0 us
    pallas_call x0 -> x1, Pallas kernels: none -> 88.6 us  [body(): pl.pallas_call(functools.partial(kernel, dims, total), out_shape=(jax.Sha...]
    all_gather x2 -> x0, waiting for transfers between devices: 85.4 us -> none  [the longest x1 85.4 us: body(): texts_whole = lax.all_gather(texts, DP_GROUP, axis=0, tiled=True)]
    all_gather x1 -> x0, blocking collectives: 50.9 us -> none  [rows_first(): filled, at, outs = (lax.all_gather(both, axis, axis=0, tiled=True), 0, [])]
    dot_general x3 -> x0, matrix products: 45.4 us -> none  [the longest x1 18.5 us: body(): lax.dot_general(col_grad.astype(jnp.bfloat16), images_whole, contract_fir...]
    psum x4 -> x0, blocking collectives: 29.9 us -> none  [one_axis_at_a_time(): value = lax.psum(value, axis)]
    reduce_sum x6 -> x0, other arithmetic: 13.1 us -> none  [the longest x1 6.49 us: body(): scale_part = jnp.sum(row_grad * row_logits)]
    all_to_all x1 -> x0, starting transfers between devices: 7.42 us -> none  [in_one_piece(): lax.all_to_all(both, axis, split_axis=split_dim, concat_axis=concat_dim,...]
    all_to_all x1 -> x0, waiting for transfers between devices: 5.9 us -> none  [in_one_piece(): lax.all_to_all(both, axis, split_axis=split_dim, concat_axis=concat_dim,...]
  transfers between devices with their start and end apart: 3 -> 0, of which waited for: 2 -> 0; matrix products, arithmetic and copies ran while one was open for 16% -> 0% of each run, Pallas kernels for 0% -> 0%
where the time goes in v1:
time: 93.6 us; the launch traced here: 93.5 us
  Pallas kernels  88.6 us (95%)
  local copies, waits for them, and re-layouts  3.53 us (4%)
  between operations  1.29 us (1%)
    pallas_call x1, Pallas kernels, body(): pl.pallas_call(functools.partial(kernel, dims, total), out_shape=(jax.Sha...  88.6 us
    unnamed x4, local copies, waits for them, and re-layouts  2.26 us

profile of v1, /device:TPU:1, one launch (start us, length us, event | category | flops | bytes accessed | tf_op | source)
XLA Modules:
  0.0 93.5 jit_solution(6960508151668440660)
XLA Ops:
  1.3 88.6 %contrastive.1 = (bf16[128,512]{1,0:T(8,128)(2,1)}, bf16[128,512]{1,0:T(8,128)(2,1)}, f32[8,128]{1,0:T(8,128)}) custom-call(f32[1]{0:T(128)} %bitcast.3.log_scale, bf16[128,512]{1,0:T(8,128)(2,1)} %images.1, bf16[128,512]{1,0:T(8,128)(2,1)} %texts.1), custom_call_target="tpu_custom_call" | custom-call | tf_op jit(solution)/shard_map/contrastive/pallas_call | solution.py:269
  89.9 1.3 %fusion = (f32[1,1]{1,0:T(1,128)}, f32[1,1]{1,0:T(1,128)}) fusion(f32[8,128]{1,0:T(8,128)} %get-tuple-element.9), kind=kLoop, calls=%fused_computation | loop fusion | bytes 16 | tf_op jit(solution)/shard_map/slice | solution.py:300
  91.2 0.0 copy-start
  91.2 1.6 %copy.10 = bf16[128,512]{1,0:T(8,128)(2,1)} copy(bf16[128,512]{1,0:T(8,128)(2,1)} %get-tuple-element.16) | data formatting | bytes 262144
  92.8 0.0 copy-done
  92.8 0.7 copy.11
Async XLA Ops:
  91.2 1.6 %copy-start = (bf16[128,512]{1,0:T(8,128)(2,1)S(1)}, bf16[128,512]{1,0:T(8,128)(2,1)}, u32[]{:S(2)}) copy-start(bf16[128,512]{1,0:T(8,128)(2,1)} %get-tuple-element.17) | copy-start | bytes 393220

commit v2 on v1

v2 whole, which is shorter than its diff:
```python
import functools
import math

import jax
import jax.numpy as jnp
from jax import lax
from jax.experimental import pallas as pl
from jax.experimental.pallas import tpu as pltpu
from jax.sharding import Mesh
from jax.sharding import PartitionSpec as P

AXES = ("x", "y", "core", "z")
CUBE = ("x", "y", "z")
MESH = pl.DeviceIdType.MESH
ROWS = 128
LOG2E = math.log2(math.e)
LN2 = math.log(2.0)
NT = (((1,), (1,)), ((), ()))


class Cube:
    def __init__(self, n):
        self.n = n
        self.order = sorted(range(2**n), key=lambda m: (bin(m).count("1"), m))
        self.pos = {m: i for i, m in enumerate(self.order)}
        self.level = {m: bin(m).count("1") for m in self.order}
        self.pieces = range(n)

    def hop(self, p, m):
        return next(k % self.n for k in range(p, p + self.n) if m >> (k % self.n) & 1)

    def children(self, p, m):
        more = [(k, m | 1 << k) for k in range(self.n) if not m >> k & 1]
        return [c for k, c in more if self.hop(p, c) == k]

    def turns(self):
        seen = []
        for q in (1, -1, 0):
            if q % self.n not in seen:
                seen.append(q % self.n)
        return seen


def cut(total, n, unit):
    units = total // unit
    ends = [-(-units * i // n) * unit for i in range(n + 1)]
    return [(a, b - a) for a, b in zip(ends, ends[1:])]


def kernel(
    dims, total,
    log_scale, images, texts,
    gi_out, gt_out, stats_out,
    X, XT, T, L, W, RM, RS, CM, CS, RL, CL, RREP, CROW,
    PI, RI, PT, RTC, RT, ST,
    local_sem, xs, xr, ts, tr, ds, dr, rls, rlr, cls, clr, pis, pir, pcs, pcr, pts, ptr, sts, str_,
):
    nd = len(dims)
    nb = 2**nd
    rows = nb * ROWS
    cube = Cube(nd)
    order, pos = cube.order, cube.pos
    me = {a: lax.axis_index(a) for a in AXES}
    core = me["core"]

    def peer(mask, kind, flip=False):
        ident = {}
        for d, a in enumerate(dims):
            if mask >> d & 1:
                c = me[a]
                ident[a] = c + 1 - 2 * (c % 2) if kind == "A" else 3 - c
        if flip:
            ident["core"] = 1 - core
        return ident

    def spot(mask, kind):
        at = 0
        for d, a in enumerate(dims):
            bit = me[a] % 2 if kind == "A" else me[a] // 2
            at = at + 2**d * (1 - bit if mask >> d & 1 else bit)
        return at

    def send(src, dst, s, r, where):
        return pltpu.make_async_remote_copy(
            src_ref=src, dst_ref=dst, send_sem=s, recv_sem=r, device_id=where, device_id_type=MESH
        )

    with jax.named_scope("enter"):
        ci = pltpu.make_async_copy(images, X.at[pl.ds(0, ROWS)], local_sem.at[0])
        ct = pltpu.make_async_copy(texts, T.at[pl.ds(0, ROWS)], local_sem.at[1])
        ci.start()
        ct.start()
        barrier = pltpu.get_barrier_semaphore()
        others = [(m, "A", False) for m in range(1, nb)]
        others += [(m, "B", f) for m in range(nb) for f in (False, True) if m or f]
        for o in others:
            pl.semaphore_signal(barrier, inc=1, device_id=peer(*o), device_id_type=MESH)
        RM[...] = jnp.full(RM.shape, -3e38, jnp.float32)
        RS[...] = jnp.zeros(RS.shape, jnp.float32)
        CM[...] = jnp.full(CM.shape, -3e38, jnp.float32)
        scale = jnp.exp(jnp.full((1, 128), log_scale[0], jnp.float32))
        scale_two = jnp.concatenate([scale * LOG2E] * 2, axis=1)
        ci.wait()
        ct.wait()
        pl.semaphore_wait(barrier, len(others))

    gp = cut(ROWS, nd, 16)
    started = []

    def go(c):
        c.start()
        started.append(c)

    def xmsg(m, p):
        k = cube.hop(p, m)
        a, n = gp[p]
        src = X.at[pl.ds(pos[m ^ 1 << k] * ROWS + a, n)]
        return send(src, X.at[pl.ds(pos[m] * ROWS + a, n)], xs.at[m, p], xr.at[m, p], peer(1 << k, "A"))

    def tmsg(m, p):
        k = cube.hop(p, m)
        a, n = gp[p]
        src = T.at[pl.ds(pos[m ^ 1 << k] * 2 * ROWS + a, n)]
        return send(src, T.at[pl.ds(pos[m] * 2 * ROWS + a, n)], ts.at[m, p], tr.at[m, p], peer(1 << k, "B"))

    def dmsg(m, p):
        a, n = gp[p]
        at = pos[m] * 2 * ROWS + a
        return send(T.at[pl.ds(at, n)], T.at[pl.ds(at + ROWS, n)], ds.at[m, p], dr.at[m, p], peer(0, "B", True))

    def pass_on(events):
        for m, p in events:
            xmsg(m, p).wait_recv()
        nxt = [(c, p) for m, p in events for c in cube.children(p, m)]
        nxt.sort(key=lambda e: not cube.children(e[1], e[0]))
        for e in nxt:
            go(xmsg(*e))
        for m, p in events:
            tmsg(m, p).wait_recv()
        for e in nxt:
            go(tmsg(*e))
        for e in events:
            go(dmsg(*e))

    def logits(r0, r1, c0, c1):
        def step(i, _):
            cols = pl.ds(pl.multiple_of(i * 256, 256), 256)
            v = lax.dot_general(X[r0:r1, :], T[cols, :], NT, preferred_element_type=jnp.float32) * scale_two
            L[r0:r1, cols] = v
            RM[r0:r1, :] = jnp.maximum(RM[r0:r1, :], jnp.maximum(v[:, :128], v[:, 128:]))
            CM[:, cols] = jnp.maximum(CM[:, cols], jnp.max(v, axis=0, keepdims=True))
            return 0

        lax.fori_loop(c0, c1, step, 0)

    def partner_texts(masks):
        for m in masks:
            for p in cube.pieces:
                dmsg(m, p).wait_recv()

    with jax.named_scope("gather"):
        for p in cube.pieces:
            go(dmsg(0, p))
        for q in cube.turns():
            for k in range(nd):
                go(xmsg(1 << k, (k + q) % nd))
                go(tmsg(1 << k, (k + q) % nd))
        groups = [[(1 << k, (k + q) % nd) for k in range(nd)] for q in cube.turns()]
        for g in groups:
            pass_on(g)
        levels = [[m for m in order if cube.level[m] == i] for i in range(nd + 1)]
    done = 0
    for lev in range(1, nd + 1):
        with jax.named_scope(f"gather{lev}"):
            have = sum(len(levels[i]) for i in range(lev))
            fresh = done
            if lev > 1:
                events = [(m, p) for m in levels[lev] for p in cube.pieces]
                deep = [e for e in events if cube.children(e[1], e[0])]
                if deep:
                    pass_on(deep)
                pass_on([e for e in events if e not in deep])
                have += len(levels[lev])
                partner_texts(levels[lev])
            else:
                have += len(levels[1])
                partner_texts(levels[0] + levels[1])
        with jax.named_scope(f"logits{lev}"):
            if done:
                logits(done * ROWS, have * ROWS, 0, done)
            logits(0, have * ROWS, done, have)
            done = have

    with jax.named_scope("sums"):
        def spread(m, _):
            at = pl.ds(pl.multiple_of(m * 128, 128), 128)
            RM[at, :] = jnp.broadcast_to(jnp.max(RM[at, :], axis=1, keepdims=True), (128, 128))
            return 0

        lax.fori_loop(0, nb, spread, 0)
        strip_rows = 256

        def sums(m, _):
            cols = pl.ds(pl.multiple_of(m * 256, 256), 256)
            cm = CM[:, cols]

            def strip(i, cs):
                at = pl.ds(pl.multiple_of(i * strip_rows, strip_rows), strip_rows)
                v = L[at, cols]
                rm = RM[at, :]
                er0 = jnp.exp2(v[:, :128] - rm)
                er1 = jnp.exp2(v[:, 128:] - rm)
                RS[at, :] = RS[at, :] + (er0 + er1)
                ec = jnp.exp2(v - cm)
                return cs + jnp.sum(ec.reshape(strip_rows // 8, 8, 256), axis=0)

            cs = lax.fori_loop(0, rows // strip_rows, strip, jnp.zeros((8, 256), jnp.float32))
            CS[:, cols] = jnp.sum(cs, axis=0, keepdims=True)
            return 0

        lax.fori_loop(0, nb, sums, 0)

    with jax.named_scope("lse"):
        ccol = CM[...] + jnp.log2(CS[...])
        for m in order:
            for f in range(2):
                at = (2 * pos[m] + f) * 128
                line = (1 - core if f else core) * nb + spot(m, "B")
                CL[0, pl.ds(line, 1), :] = ccol[:, at : at + 128]
        cc = [
            send(CL.at[0], CL.at[2 * m + f], cls.at[2 * m + f], clr.at[2 * m + f], peer(m, "B", f == 1))
            for m in reversed(order) for f in range(2) if m or f
        ]
        for c in cc:
            c.start()
        for m in order:
            at = slice(pos[m] * 128, (pos[m] + 1) * 128)
            top = jnp.max(RM[at, :].T, axis=0, keepdims=True)
            part = jnp.sum(RS[at, :].T, axis=0, keepdims=True)
            RL[0, pl.ds(spot(m, "A"), 1), :] = top + jnp.log2(part)
        rc = [send(RL.at[0], RL.at[m], rls.at[m], rlr.at[m], peer(m, "A")) for m in reversed(order[1:])]
        for c in rc:
            c.start()
    with jax.named_scope("turn"):
        XT[...] = X[...].T
        for c in started:
            c.wait_send()
    with jax.named_scope("lsewait"):
        for c in cc + rc:
            c.wait_recv()
        for c in cc + rc:
            c.wait_send()

    with jax.named_scope("join"):
        def joined(parts):
            top = functools.reduce(jnp.maximum, parts)
            return top + jnp.log2(functools.reduce(jnp.add, [jnp.exp2(p - top) for p in parts]))

        RL[0] = joined([RL[m] for m in range(nb)])
        CL[0] = joined([CL[m] for m in range(2 * nb)])
        for m in order:
            line = RL[0, pl.ds(spot(m, "A"), 1), :]
            RREP[pos[m] * 128 : (pos[m] + 1) * 128, :] = jnp.broadcast_to(line + 1.0, (128, 128)).T
            for f in range(2):
                at = (2 * pos[m] + f) * 128
                CROW[:, at : at + 128] = CL[0, pl.ds((1 - core if f else core) * nb + spot(m, "B"), 1), :] + 1.0
        eye = lax.broadcasted_iota(jnp.int32, (128, 128), 0) == lax.broadcasted_iota(jnp.int32, (128, 128), 1)
        own = L[:128, :128]
        paired = jnp.sum(jnp.where(eye, own, 0.0))
        loss_part = LN2 * (
            jnp.sum(RL[0, pl.ds(spot(0, "A"), 1), :])
            + jnp.sum(CL[0, pl.ds(core * nb + spot(0, "B"), 1), :])
            - 2.0 * paired
        )

    ip = cut(ROWS, nd, 8)
    tp = cut(XT.shape[0], nd, 8)

    def imsg(m, p):
        k = cube.hop(p, m)
        a, n = ip[p]
        at = pl.ds(pos[m] * ROWS + a, n)
        return send(PI.at[at], RI.at[at], pis.at[m, p], pir.at[m, p], peer(1 << k, "A"))

    def omsg(m, p):
        k = cube.hop(p, m)
        a, n = tp[p]
        at = pl.ds(a, n)
        return send(PT.at[0, pos[m], at], RT.at[pos[m], at], pts.at[m, p], ptr.at[m, p], peer(1 << k, "B"))

    def iadd(m, p):
        a, n = ip[p]
        v = PI[pos[m] * ROWS + a : pos[m] * ROWS + a + n, :]
        for c in cube.children(p, m):
            imsg(c, p).wait_recv()
            v = v + RI[pos[c] * ROWS + a : pos[c] * ROWS + a + n, :]
        PI[pos[m] * ROWS + a : pos[m] * ROWS + a + n, :] = v

    def oadd(m, p):
        a, n = tp[p]
        v = PT[0, pos[m], a : a + n, :]
        for c in cube.children(p, m):
            omsg(c, p).wait_recv()
            v = v + RT[pos[c], a : a + n, :]
        PT[0, pos[m], a : a + n, :] = v

    going = []

    def ready(m, msg):
        for p in cube.pieces:
            if m and not cube.children(p, m):
                c = msg(m, p)
                c.start()
                going.append(c)

    def follow(level, msg, add):
        todo = [(m, p) for m in order if cube.level[m] == level for p in cube.pieces if cube.children(p, m)]
        todo.sort(key=lambda e: len(cube.children(e[1], e[0])))
        for m, p in todo:
            add(m, p)
            if m:
                c = msg(m, p)
                c.start()
                going.append(c)

    pmsg = {
        m: send(PT.at[1, pos[m]], RTC.at[pos[m]], pcs.at[m], pcr.at[m], peer(0, "B", True)) for m in order
    }

    def pair(m):
        pmsg[m].wait_recv()
        PT[0, pos[m]] = PT[0, pos[m]] + RTC[pos[m]]
        ready(m, omsg)

    far_first = list(reversed(order))
    acc = jnp.zeros((8, 256), jnp.float32)
    behind = []
    with jax.named_scope("texts"):
        for m in far_first:
            cols = slice(pos[m] * 256, (pos[m] + 1) * 256)

            def strip(i, acc, cols=cols):
                at = pl.ds(pl.multiple_of(i * strip_rows, strip_rows), strip_rows)
                v = L[at, cols]
                rl = RREP[at, :]
                w = jnp.exp2(v - jnp.concatenate([rl, rl], axis=1)) + jnp.exp2(v - CROW[:, cols])
                W[at, cols] = w.astype(jnp.bfloat16)
                return acc + jnp.sum((w * v).reshape(strip_rows // 8, 8, 256), axis=0)

            acc = lax.fori_loop(0, rows // strip_rows, strip, acc)
            if m == 0:
                w = jnp.exp2(own - RREP[:128, :]) + jnp.exp2(own - CROW[:, :128])
                W[:128, :128] = (w - eye.astype(jnp.float32)).astype(jnp.bfloat16)
            v = jnp.dot(XT[...], W[:, cols], preferred_element_type=jnp.float32)
            PT[1, pos[m]] = v[:, 128:]
            pmsg[m].start()
            PT[0, pos[m]] = v[:, :128]
            behind.append(m)
            if len(behind) > 2:
                pair(behind.pop(0))

    line = lax.broadcasted_iota(jnp.int32, (8, 128), 0)
    scale_part = LN2 * (jnp.sum(acc) - paired)
    ST[0] = jnp.where(line == 0, loss_part, jnp.where(line == 1, scale_part, 0.0))
    stages = []
    base = 0
    for kind, masks, flip in (("A", range(1, nb), False), ("B", range(1, nb), False), ("B", (0,), True)):
        stages.append((base, [
            send(ST.at[base], ST.at[base + 1 + i], sts.at[base + i], str_.at[base + i], peer(m, kind, flip))
            for i, m in enumerate(masks)
        ]))
        base += 1 + len(masks)

    def stat(i):
        at, copies = stages[i]
        tile = ST[at]
        for j, c in enumerate(copies):
            c.wait_recv()
            tile = tile + ST[at + 1 + j]
        if i + 1 < len(stages):
            ST[stages[i + 1][0]] = tile
            for c in stages[i + 1][1]:
                c.start()
        return tile

    def image_grad(first, last):
        at = slice(first * ROWS, last * ROWS)
        PI[at, :] = jnp.dot(W[at, :], T[...], preferred_element_type=jnp.float32)

    with jax.named_scope("images"):
        for i, lev in enumerate(range(nd, -1, -1)):
            ms = levels[lev]
            image_grad(pos[ms[0]], pos[ms[-1]] + 1)
            for m in ms:
                ready(m, imsg)
            if i == 0:
                for c in stages[0][1]:
                    c.start()
                for m in behind:
                    pair(m)
    with jax.named_scope("follow"):
        for lev in range(nd - 1, 0, -1):
            follow(lev, omsg, oadd)
            follow(lev, imsg, iadd)
            if lev == nd - 1:
                stat(0)
    with jax.named_scope("last"):
        stat(1)
        follow(0, omsg, oadd)
        gt_out[...] = (PT[0, 0] * scale).T.astype(jnp.bfloat16)
        tile = stat(2)
        stats_out[...] = jnp.where(line == 0, tile * (0.5 / total), tile * (1.0 / total))
        follow(0, imsg, iadd)
        gi_out[...] = (PI[:128, :] * scale[:, :1]).astype(jnp.bfloat16)
        for c in going + list(pmsg.values()) + [c for _, cs in stages for c in cs]:
            c.wait_send()


def body(dims, total, images, texts, log_scale):
    nd = len(dims)
    nb = 2**nd
    f32, bf16 = jnp.float32, jnp.bfloat16
    vm, dma = pltpu.VMEM, pltpu.SemaphoreType.DMA
    width = images.shape[1]
    rows, cols = nb * ROWS, 2 * nb * ROWS
    gi, gt, stats = pl.pallas_call(
        functools.partial(kernel, dims, total),
        out_shape=(
            jax.ShapeDtypeStruct(images.shape, bf16),
            jax.ShapeDtypeStruct(texts.shape, bf16),
            jax.ShapeDtypeStruct((8, 128), f32),
        ),
        in_specs=[
            pl.BlockSpec(memory_space=pltpu.SMEM),
            pl.BlockSpec(memory_space=pl.ANY),
            pl.BlockSpec(memory_space=pl.ANY),
        ],
        out_specs=(pl.BlockSpec(memory_space=vm),) * 3,
        scratch_shapes=[
            vm((rows, width), bf16), vm((width, rows), bf16), vm((cols, width), bf16),
            vm((rows, cols), f32), vm((rows, cols), bf16),
            vm((rows, 128), f32), vm((rows, 128), f32), vm((1, cols), f32), vm((1, cols), f32),
            vm((nb, nb, 128), f32), vm((2 * nb, 2 * nb, 128), f32), vm((rows, 128), f32), vm((1, cols), f32),
            vm((rows, width), f32), vm((rows, width), f32),
            vm((2, nb, width, 128), f32), vm((nb, width, 128), f32), vm((nb, width, 128), f32),
            vm((2 * nb + 2, 8, 128), f32),
            dma((2,)), dma((nb, nd)), dma((nb, nd)), dma((nb, nd)), dma((nb, nd)), dma((nb, nd)), dma((nb, nd)),
            dma((nb,)), dma((nb,)), dma((2 * nb,)), dma((2 * nb,)),
            dma((nb, nd)), dma((nb, nd)), dma((nb,)), dma((nb,)), dma((nb, nd)), dma((nb, nd)),
            dma((2 * nb + 2,)), dma((2 * nb + 2,)),
        ],
        compiler_params=pltpu.CompilerParams(
            collective_id=0, has_side_effects=True, vmem_limit_bytes=60 * 2**20
        ),
        name="contrastive",
    )(log_scale.reshape(1), images, texts)
    return gi, gt, stats[0, 0], stats[1, 0]


def solution(mesh):
    return build(Mesh(mesh.devices.reshape(4, 4, 2, 4), AXES))


def build(split):
    dims = tuple(a for a in CUBE if split.shape[a] == 4)
    placed = P(AXES, None)
    return jax.shard_map(
        functools.partial(body, dims, ROWS * split.size),
        mesh=split,
        in_specs=(placed, placed, P()),
        out_specs=(placed, placed, P(), P()),
        check_vma=False,
    )
```

time: 93.6 us -> 67.7 us (0.72)
  Pallas kernels: 88.6 us -> 62.5 us
    pallas_call x1, Pallas kernels: 88.6 us -> 62.5 us  [body(): pl.pallas_call(functools.partial(kernel, dims, total), out_shape=(jax.Sha...]
where the time goes in v2:
time: 67.7 us; the launch traced here: 67.3 us
  Pallas kernels  62.5 us (92%)
  local copies, waits for them, and re-layouts  3.53 us (5%)
  between operations  1.29 us (2%)
    pallas_call x1, Pallas kernels, body(): pl.pallas_call(functools.partial(kernel, dims, total), out_shape=(jax.Sha...  62.5 us
    unnamed x4, local copies, waits for them, and re-layouts  2.26 us

profile of v2, /device:TPU:1, one launch (start us, length us, event | category | flops | bytes accessed | tf_op | source)
XLA Modules:
  0.0 67.3 jit_solution(7787976813999321218)
XLA Ops:
  1.3 62.5 %contrastive.1 = (bf16[128,512]{1,0:T(8,128)(2,1)}, bf16[128,512]{1,0:T(8,128)(2,1)}, f32[8,128]{1,0:T(8,128)}) custom-call(f32[1]{0:T(128)} %bitcast.3.log_scale, bf16[128,512]{1,0:T(8,128)(2,1)} %images.1, bf16[128,512]{1,0:T(8,128)(2,1)} %texts.1), custom_call_target="tpu_custom_call" | custom-call | tf_op jit(solution)/shard_map/contrastive/pallas_call | solution.py:426
  63.7 1.3 %fusion = (f32[1,1]{1,0:T(1,128)}, f32[1,1]{1,0:T(1,128)}) fusion(f32[8,128]{1,0:T(8,128)} %get-tuple-element.9), kind=kLoop, calls=%fused_computation | loop fusion | bytes 16 | tf_op jit(solution)/shard_map/slice | solution.py:457
  65.0 0.0 copy-start
  65.0 1.6 %copy.10 = bf16[128,512]{1,0:T(8,128)(2,1)} copy(bf16[128,512]{1,0:T(8,128)(2,1)} %get-tuple-element.16) | data formatting | bytes 262144
  66.6 0.0 copy-done
  66.6 0.7 copy.11
Async XLA Ops:
  65.0 1.6 %copy-start = (bf16[128,512]{1,0:T(8,128)(2,1)S(1)}, bf16[128,512]{1,0:T(8,128)(2,1)}, u32[]{:S(2)}) copy-start(bf16[128,512]{1,0:T(8,128)(2,1)} %get-tuple-element.17) | copy-start | bytes 393220

commit v3 on v2

--- a/solution.py
+++ b/solution.py
@@ -51,7 +51,7 @@
     dims, total,
     log_scale, images, texts,
     gi_out, gt_out, stats_out,
-    X, XT, T, L, W, RM, RS, CM, CS, RL, CL, RREP, CROW,
+    X, XT, T, L, W, RM, RN, RS, CM, CN, CS, RL, CL, RREP, CROW,
     PI, RI, PT, RTC, RT, ST,
     local_sem, xs, xr, ts, tr, ds, dr, rls, rlr, cls, clr, pis, pir, pcs, pcr, pts, ptr, sts, str_,
 ):
@@ -98,6 +98,7 @@
         RM[...] = jnp.full(RM.shape, -3e38, jnp.float32)
         RS[...] = jnp.zeros(RS.shape, jnp.float32)
         CM[...] = jnp.full(CM.shape, -3e38, jnp.float32)
+        CS[...] = jnp.zeros(CS.shape, jnp.float32)
         scale = jnp.exp(jnp.full((1, 128), log_scale[0], jnp.float32))
         scale_two = jnp.concatenate([scale * LOG2E] * 2, axis=1)
         ci.wait()
@@ -143,12 +144,37 @@
             go(dmsg(*e))
 
     def logits(r0, r1, c0, c1):
+        for i in range(c0, c1):
+            cols = slice(i * 256, (i + 1) * 256)
+            v = lax.dot_general(X[r0:r1, :], T[cols, :], NT, preferred_element_type=jnp.float32) * scale_two
+            L[r0:r1, cols] = v
+            RN[r0:r1, :] = jnp.maximum(RN[r0:r1, :], jnp.maximum(v[:, :128], v[:, 128:]))
+            CN[:, cols] = jnp.maximum(CN[:, cols], jnp.max(v, axis=0, keepdims=True))
+
+    def new_tops(r1, c1):
+        for r in range(0, r1, 128):
+            at = slice(r, r + 128)
+            top = jnp.broadcast_to(jnp.max(RN[at, :], axis=1, keepdims=True), (128, 128))
+            RS[at, :] = RS[at, :] * jnp.exp2(RM[at, :] - top)
+            RM[at, :] = top
+            RN[at, :] = top
+        cols = slice(0, c1 * 256)
+        CS[:, cols] = CS[:, cols] * jnp.exp2(CM[:, cols] - CN[:, cols])
+        CM[:, cols] = CN[:, cols]
+
+    def sums(r0, r1, c0, c1):
         def step(i, _):
             cols = pl.ds(pl.multiple_of(i * 256, 256), 256)
-            v = lax.dot_general(X[r0:r1, :], T[cols, :], NT, preferred_element_type=jnp.float32) * scale_two
-            L[r0:r1, cols] = v
-            RM[r0:r1, :] = jnp.maximum(RM[r0:r1, :], jnp.maximum(v[:, :128], v[:, 128:]))
-            CM[:, cols] = jnp.maximum(CM[:, cols], jnp.max(v, axis=0, keepdims=True))
+            cm = CM[:, cols]
+            cs = CS[:, cols]
+            for r in range(r0, r1, 64):
+                at = slice(r, r + 64)
+                v = L[at, cols]
+                rm = RM[at, :]
+                er = jnp.exp2(v[:, :128] - rm) + jnp.exp2(v[:, 128:] - rm)
+                RS[at, :] = RS[at, :] + er
+                cs = cs + jnp.sum(jnp.exp2(v - cm).reshape(8, 8, 256), axis=0)
+            CS[:, cols] = cs
             return 0
 
         lax.fori_loop(c0, c1, step, 0)
@@ -169,59 +195,35 @@
         for g in groups:
             pass_on(g)
         levels = [[m for m in order if cube.level[m] == i] for i in range(nd + 1)]
+    RN[...] = RM[...]
+    CN[...] = CM[...]
     done = 0
     for lev in range(1, nd + 1):
+        before = done
+        done = sum(len(levels[i]) for i in range(lev + 1))
+        old, new = before * ROWS, done * ROWS
         with jax.named_scope(f"gather{lev}"):
-            have = sum(len(levels[i]) for i in range(lev))
-            fresh = done
-            if lev > 1:
+            if 1 < lev < nd:
                 events = [(m, p) for m in levels[lev] for p in cube.pieces]
                 deep = [e for e in events if cube.children(e[1], e[0])]
                 if deep:
                     pass_on(deep)
                 pass_on([e for e in events if e not in deep])
-                have += len(levels[lev])
-                partner_texts(levels[lev])
-            else:
-                have += len(levels[1])
-                partner_texts(levels[0] + levels[1])
+            partner_texts((levels[0] if lev == 1 else []) + levels[lev])
         with jax.named_scope(f"logits{lev}"):
-            if done:
-                logits(done * ROWS, have * ROWS, 0, done)
-            logits(0, have * ROWS, done, have)
-            done = have
-
-    with jax.named_scope("sums"):
-        def spread(m, _):
-            at = pl.ds(pl.multiple_of(m * 128, 128), 128)
-            RM[at, :] = jnp.broadcast_to(jnp.max(RM[at, :], axis=1, keepdims=True), (128, 128))
-            return 0
-
-        lax.fori_loop(0, nb, spread, 0)
-        strip_rows = 256
-
-        def sums(m, _):
-            cols = pl.ds(pl.multiple_of(m * 256, 256), 256)
-            cm = CM[:, cols]
-
-            def strip(i, cs):
-                at = pl.ds(pl.multiple_of(i * strip_rows, strip_rows), strip_rows)
-                v = L[at, cols]
-                rm = RM[at, :]
-                er0 = jnp.exp2(v[:, :128] - rm)
-                er1 = jnp.exp2(v[:, 128:] - rm)
-                RS[at, :] = RS[at, :] + (er0 + er1)
-                ec = jnp.exp2(v - cm)
-                return cs + jnp.sum(ec.reshape(strip_rows // 8, 8, 256), axis=0)
-
-            cs = lax.fori_loop(0, rows // strip_rows, strip, jnp.zeros((8, 256), jnp.float32))
-            CS[:, cols] = jnp.sum(cs, axis=0, keepdims=True)
-            return 0
-
-        lax.fori_loop(0, nb, sums, 0)
+            if before:
+                logits(old, new, 0, before)
+            if lev == nd - 1:
+                pass_on([(m, p) for m in levels[nd] for p in cube.pieces])
+            logits(0, new, before, done)
+        with jax.named_scope(f"sums{lev}"):
+            new_tops(new, done)
+            if before:
+                sums(old, new, 0, before)
+            sums(0, new, before, done)
 
     with jax.named_scope("lse"):
-        ccol = CM[...] + jnp.log2(CS[...])
+        ccol = CM[...] + jnp.log2(jnp.sum(CS[...], axis=0, keepdims=True))
         for m in order:
             for f in range(2):
                 at = (2 * pos[m] + f) * 128
@@ -313,15 +315,16 @@
                 c.start()
                 going.append(c)
 
-    def follow(level, msg, add):
+    def follow(level):
         todo = [(m, p) for m in order if cube.level[m] == level for p in cube.pieces if cube.children(p, m)]
-        todo.sort(key=lambda e: len(cube.children(e[1], e[0])))
-        for m, p in todo:
-            add(m, p)
-            if m:
-                c = msg(m, p)
-                c.start()
-                going.append(c)
+        for n in sorted({len(cube.children(p, m)) for m, p in todo}):
+            for msg, add in ((omsg, oadd), (imsg, iadd)):
+                for m, p in todo:
+                    if len(cube.children(p, m)) == n:
+                        add(m, p)
+                        c = msg(m, p)
+                        c.start()
+                        going.append(c)
 
     pmsg = {
         m: send(PT.at[1, pos[m]], RTC.at[pos[m]], pcs.at[m], pcr.at[m], peer(0, "B", True)) for m in order
@@ -332,31 +335,36 @@
         PT[0, pos[m]] = PT[0, pos[m]] + RTC[pos[m]]
         ready(m, omsg)
 
+    def weigh(m, acc):
+        cols = slice(pos[m] * 256, (pos[m] + 1) * 256)
+        cl = CROW[:, cols]
+        for r in range(0, rows, 64):
+            at = slice(r, r + 64)
+            v = L[at, cols]
+            rl = RREP[at, :]
+            w = jnp.exp2(v - jnp.concatenate([rl, rl], axis=1)) + jnp.exp2(v - cl)
+            acc = acc + jnp.sum((w * v).reshape(8, 8, 256), axis=0)
+            if m == 0 and r < 128:
+                mark = lax.broadcasted_iota(jnp.int32, (64, 256), 0) + r == lax.broadcasted_iota(jnp.int32, (64, 256), 1)
+                w = w - mark.astype(jnp.float32)
+            W[at, cols] = w.astype(jnp.bfloat16)
+        return acc
+
     far_first = list(reversed(order))
-    acc = jnp.zeros((8, 256), jnp.float32)
     behind = []
+    with jax.named_scope("weigh"):
+        acc = weigh(far_first[0], jnp.zeros((8, 256), jnp.float32))
     with jax.named_scope("texts"):
-        for m in far_first:
+        for i, m in enumerate(far_first):
             cols = slice(pos[m] * 256, (pos[m] + 1) * 256)
-
-            def strip(i, acc, cols=cols):
-                at = pl.ds(pl.multiple_of(i * strip_rows, strip_rows), strip_rows)
-                v = L[at, cols]
-                rl = RREP[at, :]
-                w = jnp.exp2(v - jnp.concatenate([rl, rl], axis=1)) + jnp.exp2(v - CROW[:, cols])
-                W[at, cols] = w.astype(jnp.bfloat16)
-                return acc + jnp.sum((w * v).reshape(strip_rows // 8, 8, 256), axis=0)
-
-            acc = lax.fori_loop(0, rows // strip_rows, strip, acc)
-            if m == 0:
-                w = jnp.exp2(own - RREP[:128, :]) + jnp.exp2(own - CROW[:, :128])
-                W[:128, :128] = (w - eye.astype(jnp.float32)).astype(jnp.bfloat16)
             v = jnp.dot(XT[...], W[:, cols], preferred_element_type=jnp.float32)
+            if i + 1 < nb:
+                acc = weigh(far_first[i + 1], acc)
             PT[1, pos[m]] = v[:, 128:]
+            PT[0, pos[m]] = v[:, :128]
             pmsg[m].start()
-            PT[0, pos[m]] = v[:, :128]
             behind.append(m)
-            if len(behind) > 2:
+            if len(behind) > 3:
                 pair(behind.pop(0))
 
     line = lax.broadcasted_iota(jnp.int32, (8, 128), 0)
@@ -400,20 +408,28 @@
                     pair(m)
     with jax.named_scope("follow"):
         for lev in range(nd - 1, 0, -1):
-            follow(lev, omsg, oadd)
-            follow(lev, imsg, iadd)
+            follow(lev)
             if lev == nd - 1:
                 stat(0)
     with jax.named_scope("last"):
         stat(1)
-        follow(0, omsg, oadd)
+        for p in cube.pieces:
+            oadd(0, p)
         gt_out[...] = (PT[0, 0] * scale).T.astype(jnp.bfloat16)
         tile = stat(2)
         stats_out[...] = jnp.where(line == 0, tile * (0.5 / total), tile * (1.0 / total))
-        follow(0, imsg, iadd)
+        for p in cube.pieces:
+            iadd(0, p)
         gi_out[...] = (PI[:128, :] * scale[:, :1]).astype(jnp.bfloat16)
         for c in going + list(pmsg.values()) + [c for _, cs in stages for c in cs]:
             c.wait_send()
+
+
+def hand_over(gi, gt, stats, gi_out, gt_out, loss_out, scale_out):
+    gi_out[...] = gi[...]
+    gt_out[...] = gt[...]
+    loss_out[...] = stats[0:1, 0:1]
+    scale_out[...] = stats[1:2, 0:1]
 
 
 def body(dims, total, images, texts, log_scale):
@@ -439,7 +455,8 @@
         scratch_shapes=[
             vm((rows, width), bf16), vm((width, rows), bf16), vm((cols, width), bf16),
             vm((rows, cols), f32), vm((rows, cols), bf16),
-            vm((rows, 128), f32), vm((rows, 128), f32), vm((1, cols), f32), vm((1, cols), f32),
+            vm((rows, 128), f32), vm((rows, 128), f32), vm((rows, 128), f32),
+            vm((1, cols), f32), vm((1, cols), f32), vm((8, cols), f32),
             vm((nb, nb, 128), f32), vm((2 * nb, 2 * nb, 128), f32), vm((rows, 128), f32), vm((1, cols), f32),
             vm((rows, width), f32), vm((rows, width), f32),
             vm((2, nb, width, 128), f32), vm((nb, width, 128), f32), vm((nb, width, 128), f32),
@@ -454,7 +471,19 @@
         ),
         name="contrastive",
     )(log_scale.reshape(1), images, texts)
-    return gi, gt, stats[0, 0], stats[1, 0]
+    outs = pl.pallas_call(
+        hand_over,
+        out_shape=(
+            jax.ShapeDtypeStruct(images.shape, bf16),
+            jax.ShapeDtypeStruct(texts.shape, bf16),
+            jax.ShapeDtypeStruct((1, 1), f32),
+            jax.ShapeDtypeStruct((1, 1), f32),
+        ),
+        in_specs=[pl.BlockSpec(memory_space=vm)] * 3,
+        out_specs=(pl.BlockSpec(memory_space=vm),) * 4,
+        name="outputs",
+    )(gi, gt, stats)
+    return outs[0], outs[1], outs[2].reshape(()), outs[3].reshape(())
 
 
 def solution(mesh):

time: 67.7 us -> 59.9 us (0.88)
  Pallas kernels: 62.5 us -> 58.1 us
  local copies, waits for them, and re-layouts: 3.53 us -> 0 us
    pallas_call x1, Pallas kernels: 62.5 us -> 56.4 us  [body(): pl.pallas_call(functools.partial(kernel, dims, total), out_shape=(jax.Sha...]
    unnamed x4 -> x0, local copies, waits for them, and re-layouts: 2.26 us -> none
    pallas_call x0 -> x1, Pallas kernels: none -> 1.68 us  [body(): pl.pallas_call(hand_over, out_shape=(jax.ShapeDtypeStruct(images.shape, b...]
    slice x1 -> x0, local copies, waits for them, and re-layouts: 1.27 us -> none  [body(): return (gi, gt, stats[0, 0], stats[1, 0])]
where the time goes in v3:
time: 59.9 us; the launch traced here: 59.4 us
  Pallas kernels  58.1 us (97%)
  between operations  1.29 us (2%)
    pallas_call x1, Pallas kernels, body(): pl.pallas_call(functools.partial(kernel, dims, total), out_shape=(jax.Sha...  56.4 us
    pallas_call x1, Pallas kernels, body(): pl.pallas_call(hand_over, out_shape=(jax.ShapeDtypeStruct(images.shape, b...  1.68 us

profile of v3, /device:TPU:1, one launch (start us, length us, event | category | flops | bytes accessed | tf_op | source)
XLA Modules:
  0.0 59.4 jit_solution(11341283169745811186)
XLA Ops:
  1.3 56.4 %contrastive.1 = (bf16[128,512]{1,0:T(8,128)(2,1)}, bf16[128,512]{1,0:T(8,128)(2,1)}, f32[8,128]{1,0:T(8,128)}) custom-call(f32[1]{0:T(128)} %bitcast.3.log_scale, bf16[128,512]{1,0:T(8,128)(2,1)} %images.1, bf16[128,512]{1,0:T(8,128)(2,1)} %texts.1), custom_call_target="tpu_custom_call" | custom-call | tf_op jit(solution)/shard_map/contrastive/pallas_call | solution.py:442
  57.7 1.7 %outputs.1 = (bf16[128,512]{1,0:T(8,128)(2,1)}, bf16[128,512]{1,0:T(8,128)(2,1)}, f32[1,1]{1,0:T(1,128)}, f32[1,1]{1,0:T(1,128)}) custom-call(bf16[128,512]{1,0:T(8,128)(2,1)} %get-tuple-element.11.gi, bf16[128,512]{1,0:T(8,128)(2,1)} %get-tuple-element.12.gt, f32[8,128]{1,0:T(8,128)} %get-tuple-element.13.stats), custom_call_target="tpu_custom_call" | custom-call | tf_op jit(solution)/shard_map/outputs/pallas_call | solution.py:474

commit v4 on v3

--- a/solution.py
+++ b/solution.py
@@ -51,7 +51,7 @@
     dims, total,
     log_scale, images, texts,
     gi_out, gt_out, stats_out,
-    X, XT, T, L, W, RM, RN, RS, CM, CN, CS, RL, CL, RREP, CROW,
+    X, XT, T, L, W, RM, RN, RS, UR, CM, CN, CS, UC, RL, CL, RREP, CROW,
     PI, RI, PT, RTC, RT, ST,
     local_sem, xs, xr, ts, tr, ds, dr, rls, rlr, cls, clr, pis, pir, pcs, pcr, pts, ptr, sts, str_,
 ):
@@ -68,7 +68,7 @@
         for d, a in enumerate(dims):
             if mask >> d & 1:
                 c = me[a]
-                ident[a] = c + 1 - 2 * (c % 2) if kind == "A" else 3 - c
+                ident[a] = 3 - c if kind == "A" else c + 1 - 2 * (c % 2)
         if flip:
             ident["core"] = 1 - core
         return ident
@@ -76,7 +76,7 @@
     def spot(mask, kind):
         at = 0
         for d, a in enumerate(dims):
-            bit = me[a] % 2 if kind == "A" else me[a] // 2
+            bit = me[a] // 2 if kind == "A" else me[a] % 2
             at = at + 2**d * (1 - bit if mask >> d & 1 else bit)
         return at
 
@@ -91,14 +91,15 @@
         ci.start()
         ct.start()
         barrier = pltpu.get_barrier_semaphore()
-        others = [(m, "A", False) for m in range(1, nb)]
-        others += [(m, "B", f) for m in range(nb) for f in (False, True) if m or f]
+        others = [(1 << k, kind, False) for k in range(nd) for kind in "AB"] + [(0, "B", True)]
         for o in others:
             pl.semaphore_signal(barrier, inc=1, device_id=peer(*o), device_id_type=MESH)
         RM[...] = jnp.full(RM.shape, -3e38, jnp.float32)
         RS[...] = jnp.zeros(RS.shape, jnp.float32)
         CM[...] = jnp.full(CM.shape, -3e38, jnp.float32)
         CS[...] = jnp.zeros(CS.shape, jnp.float32)
+        UR[...] = jnp.zeros(UR.shape, jnp.float32)
+        UC[...] = jnp.zeros(UC.shape, jnp.float32)
         scale = jnp.exp(jnp.full((1, 128), log_scale[0], jnp.float32))
         scale_two = jnp.concatenate([scale * LOG2E] * 2, axis=1)
         ci.wait()
@@ -155,11 +156,15 @@
         for r in range(0, r1, 128):
             at = slice(r, r + 128)
             top = jnp.broadcast_to(jnp.max(RN[at, :], axis=1, keepdims=True), (128, 128))
-            RS[at, :] = RS[at, :] * jnp.exp2(RM[at, :] - top)
+            fall = jnp.exp2(RM[at, :] - top)
+            RS[at, :] = RS[at, :] * fall
+            UR[at, :] = UR[at, :] * fall
             RM[at, :] = top
             RN[at, :] = top
         cols = slice(0, c1 * 256)
-        CS[:, cols] = CS[:, cols] * jnp.exp2(CM[:, cols] - CN[:, cols])
+        fall = jnp.exp2(CM[:, cols] - CN[:, cols])
+        CS[:, cols] = CS[:, cols] * fall
+        UC[:, cols] = UC[:, cols] * fall
         CM[:, cols] = CN[:, cols]
 
     def sums(r0, r1, c0, c1):
@@ -167,14 +172,20 @@
             cols = pl.ds(pl.multiple_of(i * 256, 256), 256)
             cm = CM[:, cols]
             cs = CS[:, cols]
+            uc = UC[:, cols]
             for r in range(r0, r1, 64):
                 at = slice(r, r + 64)
                 v = L[at, cols]
                 rm = RM[at, :]
-                er = jnp.exp2(v[:, :128] - rm) + jnp.exp2(v[:, 128:] - rm)
-                RS[at, :] = RS[at, :] + er
-                cs = cs + jnp.sum(jnp.exp2(v - cm).reshape(8, 8, 256), axis=0)
+                er0 = jnp.exp2(v[:, :128] - rm)
+                er1 = jnp.exp2(v[:, 128:] - rm)
+                RS[at, :] = RS[at, :] + (er0 + er1)
+                UR[at, :] = UR[at, :] + (er0 * v[:, :128] + er1 * v[:, 128:])
+                ec = jnp.exp2(v - cm)
+                cs = cs + jnp.sum(ec.reshape(8, 8, 256), axis=0)
+                uc = uc + jnp.sum((ec * v).reshape(8, 8, 256), axis=0)
             CS[:, cols] = cs
+            UC[:, cols] = uc
             return 0
 
         lax.fori_loop(c0, c1, step, 0)
@@ -213,13 +224,13 @@
         with jax.named_scope(f"logits{lev}"):
             if before:
                 logits(old, new, 0, before)
-            if lev == nd - 1:
-                pass_on([(m, p) for m in levels[nd] for p in cube.pieces])
             logits(0, new, before, done)
         with jax.named_scope(f"sums{lev}"):
             new_tops(new, done)
             if before:
                 sums(old, new, 0, before)
+            if lev == nd - 1:
+                pass_on([(m, p) for m in levels[nd] for p in cube.pieces])
             sums(0, new, before, done)
 
     with jax.named_scope("lse"):
@@ -267,13 +278,10 @@
                 at = (2 * pos[m] + f) * 128
                 CROW[:, at : at + 128] = CL[0, pl.ds((1 - core if f else core) * nb + spot(m, "B"), 1), :] + 1.0
         eye = lax.broadcasted_iota(jnp.int32, (128, 128), 0) == lax.broadcasted_iota(jnp.int32, (128, 128), 1)
-        own = L[:128, :128]
-        paired = jnp.sum(jnp.where(eye, own, 0.0))
-        loss_part = LN2 * (
-            jnp.sum(RL[0, pl.ds(spot(0, "A"), 1), :])
-            + jnp.sum(CL[0, pl.ds(core * nb + spot(0, "B"), 1), :])
-            - 2.0 * paired
-        )
+        paired = jnp.sum(jnp.where(eye, L[:128, :128], 0.0).reshape(16, 8, 128), axis=0)
+        line = lax.broadcasted_iota(jnp.int32, (8, 128), 0)
+        own = RL[0, pl.ds(spot(0, "A"), 1), :] + CL[0, pl.ds(core * nb + spot(0, "B"), 1), :]
+        loss_part = jnp.where(line == 0, own, 0.0) - 2.0 * paired
 
     ip = cut(ROWS, nd, 8)
     tp = cut(XT.shape[0], nd, 8)
@@ -315,10 +323,10 @@
                 c.start()
                 going.append(c)
 
-    def follow(level):
+    def follow(level, which):
         todo = [(m, p) for m in order if cube.level[m] == level for p in cube.pieces if cube.children(p, m)]
         for n in sorted({len(cube.children(p, m)) for m, p in todo}):
-            for msg, add in ((omsg, oadd), (imsg, iadd)):
+            for msg, add in [{"o": (omsg, oadd), "i": (imsg, iadd)}[w] for w in which]:
                 for m, p in todo:
                     if len(cube.children(p, m)) == n:
                         add(m, p)
@@ -335,93 +343,101 @@
         PT[0, pos[m]] = PT[0, pos[m]] + RTC[pos[m]]
         ready(m, omsg)
 
-    def weigh(m, acc):
+    def weigh(r0, r1, c0, c1):
+        for c in range(c0, c1):
+            cols = slice(c * 256, (c + 1) * 256)
+            cl = CROW[:, cols]
+            for r in range(r0, r1, 64):
+                at = slice(r, r + 64)
+                v = L[at, cols]
+                rl = RREP[at, :]
+                w = jnp.exp2(v - jnp.concatenate([rl, rl], axis=1)) + jnp.exp2(v - cl)
+                if c == 0 and r < 128:
+                    across = lax.broadcasted_iota(jnp.int32, (64, 256), 1)
+                    mark = lax.broadcasted_iota(jnp.int32, (64, 256), 0) + r == across
+                    w = w - mark.astype(jnp.float32)
+                W[at, cols] = w.astype(jnp.bfloat16)
+
+    def text_grad(m):
         cols = slice(pos[m] * 256, (pos[m] + 1) * 256)
-        cl = CROW[:, cols]
-        for r in range(0, rows, 64):
-            at = slice(r, r + 64)
-            v = L[at, cols]
-            rl = RREP[at, :]
-            w = jnp.exp2(v - jnp.concatenate([rl, rl], axis=1)) + jnp.exp2(v - cl)
-            acc = acc + jnp.sum((w * v).reshape(8, 8, 256), axis=0)
-            if m == 0 and r < 128:
-                mark = lax.broadcasted_iota(jnp.int32, (64, 256), 0) + r == lax.broadcasted_iota(jnp.int32, (64, 256), 1)
-                w = w - mark.astype(jnp.float32)
-            W[at, cols] = w.astype(jnp.bfloat16)
-        return acc
-
-    far_first = list(reversed(order))
-    behind = []
-    with jax.named_scope("weigh"):
-        acc = weigh(far_first[0], jnp.zeros((8, 256), jnp.float32))
-    with jax.named_scope("texts"):
-        for i, m in enumerate(far_first):
-            cols = slice(pos[m] * 256, (pos[m] + 1) * 256)
-            v = jnp.dot(XT[...], W[:, cols], preferred_element_type=jnp.float32)
-            if i + 1 < nb:
-                acc = weigh(far_first[i + 1], acc)
-            PT[1, pos[m]] = v[:, 128:]
-            PT[0, pos[m]] = v[:, :128]
-            pmsg[m].start()
-            behind.append(m)
-            if len(behind) > 3:
-                pair(behind.pop(0))
-
-    line = lax.broadcasted_iota(jnp.int32, (8, 128), 0)
-    scale_part = LN2 * (jnp.sum(acc) - paired)
-    ST[0] = jnp.where(line == 0, loss_part, jnp.where(line == 1, scale_part, 0.0))
-    stages = []
-    base = 0
-    for kind, masks, flip in (("A", range(1, nb), False), ("B", range(1, nb), False), ("B", (0,), True)):
-        stages.append((base, [
-            send(ST.at[base], ST.at[base + 1 + i], sts.at[base + i], str_.at[base + i], peer(m, kind, flip))
-            for i, m in enumerate(masks)
-        ]))
-        base += 1 + len(masks)
-
-    def stat(i):
-        at, copies = stages[i]
+        v = jnp.dot(XT[...], W[:, cols], preferred_element_type=jnp.float32)
+        PT[1, pos[m]] = v[:, 128:]
+        PT[0, pos[m]] = v[:, :128]
+        pmsg[m].start()
+
+    def image_grad(first, last):
+        at = slice(first * ROWS, last * ROWS)
+        PI[at, :] = jnp.dot(W[at, :], T[...], preferred_element_type=jnp.float32)
+
+    far = [(m, f) for m in range(nb) for f in (False, True) if m or f]
+    stages = [
+        [send(ST.at[0], ST.at[m], sts.at[m], str_.at[m], peer(m, "A")) for m in range(1, nb)],
+        [send(ST.at[nb], ST.at[nb + 1 + i], sts.at[nb + i], str_.at[nb + i], peer(m, "B", f)) for i, (m, f) in enumerate(far)],
+    ]
+
+    def stat(at, copies):
         tile = ST[at]
         for j, c in enumerate(copies):
             c.wait_recv()
             tile = tile + ST[at + 1 + j]
-        if i + 1 < len(stages):
-            ST[stages[i + 1][0]] = tile
-            for c in stages[i + 1][1]:
-                c.start()
         return tile
 
-    def image_grad(first, last):
-        at = slice(first * ROWS, last * ROWS)
-        PI[at, :] = jnp.dot(W[at, :], T[...], preferred_element_type=jnp.float32)
-
-    with jax.named_scope("images"):
-        for i, lev in enumerate(range(nd, -1, -1)):
-            ms = levels[lev]
-            image_grad(pos[ms[0]], pos[ms[-1]] + 1)
-            for m in ms:
+    with jax.named_scope("scalars"):
+        part = -paired
+        for r in range(0, rows, 128):
+            at = slice(r, r + 128)
+            part = part + jnp.sum((UR[at, :] * jnp.exp2(RM[at, :] - RREP[at, :])).reshape(16, 8, 128), axis=0)
+        both = UC[...] * jnp.exp2(CM[...] - CROW[...])
+        for c in range(0, 2 * rows, 128):
+            part = part + both[:, c : c + 128]
+        ST[0, :8] = loss_part
+        ST[0, 8:] = part
+        for c in stages[0]:
+            c.start()
+    waiting = []
+    for lev in range(nd, -1, -1):
+        first, last = pos[levels[lev][0]], pos[levels[lev][-1]] + 1
+        low = 0 if lev == 1 else first
+        with jax.named_scope(f"texts{lev}"):
+            if lev:
+                weigh(0, last * ROWS, low, last)
+            for m in levels[lev]:
+                text_grad(m)
+                for w in waiting:
+                    pair(w)
+                waiting = []
+            waiting = list(levels[lev])
+        if lev == 1:
+            with jax.named_scope("stats"):
+                ST[nb] = stat(0, stages[0])
+                for c in stages[1]:
+                    c.start()
+        with jax.named_scope(f"images{lev}"):
+            if lev > 1:
+                weigh(first * ROWS, last * ROWS, 0, first)
+            image_grad(first, last)
+            if lev == 1 < nd:
+                follow(nd - 1, "i")
+            for m in levels[lev]:
                 ready(m, imsg)
-            if i == 0:
-                for c in stages[0][1]:
-                    c.start()
-                for m in behind:
-                    pair(m)
+            if lev == 1 < nd:
+                follow(nd - 1, "o")
+    pair(0)
     with jax.named_scope("follow"):
-        for lev in range(nd - 1, 0, -1):
-            follow(lev)
-            if lev == nd - 1:
-                stat(0)
+        for lev in range(nd - 2, 0, -1):
+            follow(lev, "oi")
     with jax.named_scope("last"):
-        stat(1)
         for p in cube.pieces:
             oadd(0, p)
         gt_out[...] = (PT[0, 0] * scale).T.astype(jnp.bfloat16)
-        tile = stat(2)
-        stats_out[...] = jnp.where(line == 0, tile * (0.5 / total), tile * (1.0 / total))
         for p in cube.pieces:
             iadd(0, p)
         gi_out[...] = (PI[:128, :] * scale[:, :1]).astype(jnp.bfloat16)
-        for c in going + list(pmsg.values()) + [c for _, cs in stages for c in cs]:
+        tile = stat(nb, stages[1])
+        loss = jnp.sum(tile[:8]) * (LN2 * 0.5 / total)
+        grad_scale = jnp.sum(tile[8:]) * (LN2 / total)
+        stats_out[...] = jnp.where(line == 0, loss, grad_scale)
+        for c in going + list(pmsg.values()) + stages[0] + stages[1]:
             c.wait_send()
 
 
@@ -455,16 +471,16 @@
         scratch_shapes=[
             vm((rows, width), bf16), vm((width, rows), bf16), vm((cols, width), bf16),
             vm((rows, cols), f32), vm((rows, cols), bf16),
-            vm((rows, 128), f32), vm((rows, 128), f32), vm((rows, 128), f32),
-            vm((1, cols), f32), vm((1, cols), f32), vm((8, cols), f32),
+            vm((rows, 128), f32), vm((rows, 128), f32), vm((rows, 128), f32), vm((rows, 128), f32),
+            vm((1, cols), f32), vm((1, cols), f32), vm((8, cols), f32), vm((8, cols), f32),
             vm((nb, nb, 128), f32), vm((2 * nb, 2 * nb, 128), f32), vm((rows, 128), f32), vm((1, cols), f32),
             vm((rows, width), f32), vm((rows, width), f32),
             vm((2, nb, width, 128), f32), vm((nb, width, 128), f32), vm((nb, width, 128), f32),
-            vm((2 * nb + 2, 8, 128), f32),
+            vm((3 * nb, 16, 128), f32),
             dma((2,)), dma((nb, nd)), dma((nb, nd)), dma((nb, nd)), dma((nb, nd)), dma((nb, nd)), dma((nb, nd)),
             dma((nb,)), dma((nb,)), dma((2 * nb,)), dma((2 * nb,)),
             dma((nb, nd)), dma((nb, nd)), dma((nb,)), dma((nb,)), dma((nb, nd)), dma((nb, nd)),
-            dma((2 * nb + 2,)), dma((2 * nb + 2,)),
+            dma((3 * nb,)), dma((3 * nb,)),
         ],
         compiler_params=pltpu.CompilerParams(
             collective_id=0, has_side_effects=True, vmem_limit_bytes=60 * 2**20

time: 59.9 us -> 55.4 us (0.925)
  Pallas kernels: 58.1 us -> 53.9 us
    pallas_call x1, Pallas kernels: 56.4 us -> 52.3 us  [body(): pl.pallas_call(functools.partial(kernel, dims, total), out_shape=(jax.Sha...]
where the time goes in v4:
time: 55.4 us; the launch traced here: 55.2 us
  Pallas kernels  53.9 us (97%)
  between operations  1.29 us (2%)
    pallas_call x1, Pallas kernels, body(): pl.pallas_call(functools.partial(kernel, dims, total), out_shape=(jax.Sha...  52.3 us
    pallas_call x1, Pallas kernels, body(): pl.pallas_call(hand_over, out_shape=(jax.ShapeDtypeStruct(images.shape, b...  1.68 us

profile of v4, /device:TPU:1, one launch (start us, length us, event | category | flops | bytes accessed | tf_op | source)
XLA Modules:
  0.0 55.2 jit_solution(3331155595027538591)
XLA Ops:
  1.3 52.3 %contrastive.1 = (bf16[128,512]{1,0:T(8,128)(2,1)}, bf16[128,512]{1,0:T(8,128)(2,1)}, f32[8,128]{1,0:T(8,128)}) custom-call(f32[1]{0:T(128)} %bitcast.3.log_scale, bf16[128,512]{1,0:T(8,128)(2,1)} %images.1, bf16[128,512]{1,0:T(8,128)(2,1)} %texts.1), custom_call_target="tpu_custom_call" | custom-call | tf_op jit(solution)/shard_map/contrastive/pallas_call | solution.py:458
  53.5 1.7 %outputs.1 = (bf16[128,512]{1,0:T(8,128)(2,1)}, bf16[128,512]{1,0:T(8,128)(2,1)}, f32[1,1]{1,0:T(1,128)}, f32[1,1]{1,0:T(1,128)}) custom-call(bf16[128,512]{1,0:T(8,128)(2,1)} %get-tuple-element.11.gi, bf16[128,512]{1,0:T(8,128)(2,1)} %get-tuple-element.12.gt, f32[8,128]{1,0:T(8,128)} %get-tuple-element.13.stats), custom_call_target="tpu_custom_call" | custom-call | tf_op jit(solution)/shard_map/outputs/pallas_call | solution.py:490

commit v5 on v4

--- a/solution.py
+++ b/solution.py
@@ -99,7 +99,6 @@
         CM[...] = jnp.full(CM.shape, -3e38, jnp.float32)
         CS[...] = jnp.zeros(CS.shape, jnp.float32)
         UR[...] = jnp.zeros(UR.shape, jnp.float32)
-        UC[...] = jnp.zeros(UC.shape, jnp.float32)
         scale = jnp.exp(jnp.full((1, 128), log_scale[0], jnp.float32))
         scale_two = jnp.concatenate([scale * LOG2E] * 2, axis=1)
         ci.wait()
@@ -156,15 +155,11 @@
         for r in range(0, r1, 128):
             at = slice(r, r + 128)
             top = jnp.broadcast_to(jnp.max(RN[at, :], axis=1, keepdims=True), (128, 128))
-            fall = jnp.exp2(RM[at, :] - top)
-            RS[at, :] = RS[at, :] * fall
-            UR[at, :] = UR[at, :] * fall
+            RS[at, :] = RS[at, :] * jnp.exp2(RM[at, :] - top)
             RM[at, :] = top
             RN[at, :] = top
         cols = slice(0, c1 * 256)
-        fall = jnp.exp2(CM[:, cols] - CN[:, cols])
-        CS[:, cols] = CS[:, cols] * fall
-        UC[:, cols] = UC[:, cols] * fall
+        CS[:, cols] = CS[:, cols] * jnp.exp2(CM[:, cols] - CN[:, cols])
         CM[:, cols] = CN[:, cols]
 
     def sums(r0, r1, c0, c1):
@@ -172,7 +167,6 @@
             cols = pl.ds(pl.multiple_of(i * 256, 256), 256)
             cm = CM[:, cols]
             cs = CS[:, cols]
-            uc = UC[:, cols]
             for r in range(r0, r1, 64):
                 at = slice(r, r + 64)
                 v = L[at, cols]
@@ -180,12 +174,9 @@
                 er0 = jnp.exp2(v[:, :128] - rm)
                 er1 = jnp.exp2(v[:, 128:] - rm)
                 RS[at, :] = RS[at, :] + (er0 + er1)
-                UR[at, :] = UR[at, :] + (er0 * v[:, :128] + er1 * v[:, 128:])
                 ec = jnp.exp2(v - cm)
                 cs = cs + jnp.sum(ec.reshape(8, 8, 256), axis=0)
-                uc = uc + jnp.sum((ec * v).reshape(8, 8, 256), axis=0)
             CS[:, cols] = cs
-            UC[:, cols] = uc
             return 0
 
         lax.fori_loop(c0, c1, step, 0)
@@ -255,6 +246,22 @@
         for c in rc:
             c.start()
     with jax.named_scope("turn"):
+        def tilt(c, _):
+            cols = pl.ds(pl.multiple_of(c * 256, 256), 256)
+            cm = CM[:, cols]
+
+            def strip(i, uc):
+                at = pl.ds(pl.multiple_of(i * 256, 256), 256)
+                v = L[at, cols]
+                rm = RM[at, :]
+                v0, v1 = v[:, :128], v[:, 128:]
+                UR[at, :] = UR[at, :] + (jnp.exp2(v0 - rm) * v0 + jnp.exp2(v1 - rm) * v1)
+                return uc + jnp.sum((jnp.exp2(v - cm) * v).reshape(32, 8, 256), axis=0)
+
+            UC[:, cols] = lax.fori_loop(0, rows // 256, strip, jnp.zeros((8, 256), jnp.float32))
+            return 0
+
+        lax.fori_loop(0, nb, tilt, 0)
         XT[...] = X[...].T
         for c in started:
             c.wait_send()
@@ -406,7 +413,6 @@
                 for w in waiting:
                     pair(w)
                 waiting = []
-            waiting = list(levels[lev])
         if lev == 1:
             with jax.named_scope("stats"):
                 ST[nb] = stat(0, stages[0])
@@ -422,7 +428,11 @@
                 ready(m, imsg)
             if lev == 1 < nd:
                 follow(nd - 1, "o")
-    pair(0)
+            if lev == nd:
+                waiting = list(levels[lev])
+            else:
+                for m in levels[lev]:
+                    pair(m)
     with jax.named_scope("follow"):
         for lev in range(nd - 2, 0, -1):
             follow(lev, "oi")

time: 55.4 us -> 54.3 us (0.980)
  Pallas kernels: 53.9 us -> 52.9 us
    pallas_call x1, Pallas kernels: 52.3 us -> 51.2 us  [body(): pl.pallas_call(functools.partial(kernel, dims, total), out_shape=(jax.Sha...]
where the time goes in v5:
time: 54.3 us; the launch traced here: 54.2 us
  Pallas kernels  52.9 us (97%)
  between operations  1.29 us (2%)
    pallas_call x1, Pallas kernels, body(): pl.pallas_call(functools.partial(kernel, dims, total), out_shape=(jax.Sha...  51.2 us
    pallas_call x1, Pallas kernels, body(): pl.pallas_call(hand_over, out_shape=(jax.ShapeDtypeStruct(images.shape, b...  1.68 us

profile of v5, /device:TPU:1, one launch (start us, length us, event | category | flops | bytes accessed | tf_op | source)
XLA Modules:
  0.0 54.2 jit_solution(12102280001164895028)
XLA Ops:
  1.3 51.2 %contrastive.1 = (bf16[128,512]{1,0:T(8,128)(2,1)}, bf16[128,512]{1,0:T(8,128)(2,1)}, f32[8,128]{1,0:T(8,128)}) custom-call(f32[1]{0:T(128)} %bitcast.3.log_scale, bf16[128,512]{1,0:T(8,128)(2,1)} %images.1, bf16[128,512]{1,0:T(8,128)(2,1)} %texts.1), custom_call_target="tpu_custom_call" | custom-call | tf_op jit(solution)/shard_map/contrastive/pallas_call | solution.py:468
  52.5 1.7 %outputs.1 = (bf16[128,512]{1,0:T(8,128)(2,1)}, bf16[128,512]{1,0:T(8,128)(2,1)}, f32[1,1]{1,0:T(1,128)}, f32[1,1]{1,0:T(1,128)}) custom-call(bf16[128,512]{1,0:T(8,128)(2,1)} %get-tuple-element.11.gi, bf16[128,512]{1,0:T(8,128)(2,1)} %get-tuple-element.12.gt, f32[8,128]{1,0:T(8,128)} %get-tuple-element.13.stats), custom_call_target="tpu_custom_call" | custom-call | tf_op jit(solution)/shard_map/outputs/pallas_call | solution.py:500

commit v6 on v5

--- a/solution.py
+++ b/solution.py
@@ -99,7 +99,7 @@
         CM[...] = jnp.full(CM.shape, -3e38, jnp.float32)
         CS[...] = jnp.zeros(CS.shape, jnp.float32)
         UR[...] = jnp.zeros(UR.shape, jnp.float32)
-        scale = jnp.exp(jnp.full((1, 128), log_scale[0], jnp.float32))
+        scale = jnp.exp(jnp.full((1, 128), log_scale[()], jnp.float32))
         scale_two = jnp.concatenate([scale * LOG2E] * 2, axis=1)
         ci.wait()
         ct.wait()
@@ -149,16 +149,13 @@
             v = lax.dot_general(X[r0:r1, :], T[cols, :], NT, preferred_element_type=jnp.float32) * scale_two
             L[r0:r1, cols] = v
             RN[r0:r1, :] = jnp.maximum(RN[r0:r1, :], jnp.maximum(v[:, :128], v[:, 128:]))
-            CN[:, cols] = jnp.maximum(CN[:, cols], jnp.max(v, axis=0, keepdims=True))
-
-    def new_tops(r1, c1):
-        for r in range(0, r1, 128):
-            at = slice(r, r + 128)
-            top = jnp.broadcast_to(jnp.max(RN[at, :], axis=1, keepdims=True), (128, 128))
-            RS[at, :] = RS[at, :] * jnp.exp2(RM[at, :] - top)
-            RM[at, :] = top
-            RN[at, :] = top
-        cols = slice(0, c1 * 256)
+            CN[:, cols] = jnp.maximum(CN[:, cols], jnp.max(v.reshape(-1, 8, 256), axis=0))
+
+    def new_tops(r0, r1, c0, c1):
+        at = slice(r0, r1)
+        RS[at, :] = RS[at, :] * jnp.exp2(RM[at, :] - RN[at, :])
+        RM[at, :] = RN[at, :]
+        cols = slice(c0 * 256, c1 * 256)
         CS[:, cols] = CS[:, cols] * jnp.exp2(CM[:, cols] - CN[:, cols])
         CM[:, cols] = CN[:, cols]
 
@@ -174,8 +171,8 @@
                 er0 = jnp.exp2(v[:, :128] - rm)
                 er1 = jnp.exp2(v[:, 128:] - rm)
                 RS[at, :] = RS[at, :] + (er0 + er1)
-                ec = jnp.exp2(v - cm)
-                cs = cs + jnp.sum(ec.reshape(8, 8, 256), axis=0)
+                ec = jnp.exp2(v.reshape(8, 8, 256) - cm)
+                cs = cs + jnp.sum(ec, axis=0)
             CS[:, cols] = cs
             return 0
 
@@ -193,16 +190,19 @@
             for k in range(nd):
                 go(xmsg(1 << k, (k + q) % nd))
                 go(tmsg(1 << k, (k + q) % nd))
+        levels = [[m for m in order if cube.level[m] == i] for i in range(nd + 1)]
+        RN[...] = RM[...]
+        CN[...] = CM[...]
+        partner_texts(levels[0])
+        logits(0, ROWS, 0, 1)
+        new_tops(0, ROWS, 0, 1)
+        sums(0, ROWS, 0, 1)
         groups = [[(1 << k, (k + q) % nd) for k in range(nd)] for q in cube.turns()]
         for g in groups:
             pass_on(g)
-        levels = [[m for m in order if cube.level[m] == i] for i in range(nd + 1)]
-    RN[...] = RM[...]
-    CN[...] = CM[...]
-    done = 0
     for lev in range(1, nd + 1):
-        before = done
-        done = sum(len(levels[i]) for i in range(lev + 1))
+        before = sum(len(levels[i]) for i in range(lev))
+        done = before + len(levels[lev])
         old, new = before * ROWS, done * ROWS
         with jax.named_scope(f"gather{lev}"):
             if 1 < lev < nd:
@@ -211,21 +211,22 @@
                 if deep:
                     pass_on(deep)
                 pass_on([e for e in events if e not in deep])
-            partner_texts((levels[0] if lev == 1 else []) + levels[lev])
-        with jax.named_scope(f"logits{lev}"):
-            if before:
-                logits(old, new, 0, before)
+            elif lev > 1:
+                pass_on([(m, p) for m in levels[lev] for p in cube.pieces])
+        with jax.named_scope(f"rows{lev}"):
+            logits(old, new, 0, before)
+            new_tops(old, new, 0, before)
+            sums(old, new, 0, before)
+        with jax.named_scope(f"partner{lev}"):
+            partner_texts(levels[lev])
+        with jax.named_scope(f"columns{lev}"):
             logits(0, new, before, done)
-        with jax.named_scope(f"sums{lev}"):
-            new_tops(new, done)
-            if before:
-                sums(old, new, 0, before)
-            if lev == nd - 1:
-                pass_on([(m, p) for m in levels[nd] for p in cube.pieces])
+            new_tops(0, new, before, done)
             sums(0, new, before, done)
 
     with jax.named_scope("lse"):
-        ccol = CM[...] + jnp.log2(jnp.sum(CS[...], axis=0, keepdims=True))
+        ctop = jnp.max(CM[...], axis=0, keepdims=True)
+        ccol = ctop + jnp.log2(jnp.sum(CS[...] * jnp.exp2(CM[...] - ctop), axis=0, keepdims=True))
         for m in order:
             for f in range(2):
                 at = (2 * pos[m] + f) * 128
@@ -239,8 +240,9 @@
             c.start()
         for m in order:
             at = slice(pos[m] * 128, (pos[m] + 1) * 128)
-            top = jnp.max(RM[at, :].T, axis=0, keepdims=True)
-            part = jnp.sum(RS[at, :].T, axis=0, keepdims=True)
+            tops = RM[at, :].T
+            top = jnp.max(tops, axis=0, keepdims=True)
+            part = jnp.sum(RS[at, :].T * jnp.exp2(tops - top), axis=0, keepdims=True)
             RL[0, pl.ds(spot(m, "A"), 1), :] = top + jnp.log2(part)
         rc = [send(RL.at[0], RL.at[m], rls.at[m], rlr.at[m], peer(m, "A")) for m in reversed(order[1:])]
         for c in rc:
@@ -256,7 +258,8 @@
                 rm = RM[at, :]
                 v0, v1 = v[:, :128], v[:, 128:]
                 UR[at, :] = UR[at, :] + (jnp.exp2(v0 - rm) * v0 + jnp.exp2(v1 - rm) * v1)
-                return uc + jnp.sum((jnp.exp2(v - cm) * v).reshape(32, 8, 256), axis=0)
+                w = v.reshape(32, 8, 256)
+                return uc + jnp.sum(jnp.exp2(w - cm) * w, axis=0)
 
             UC[:, cols] = lax.fori_loop(0, rows // 256, strip, jnp.zeros((8, 256), jnp.float32))
             return 0
@@ -389,7 +392,7 @@
             tile = tile + ST[at + 1 + j]
         return tile
 
-    with jax.named_scope("scalars"):
+    def spread_scalars():
         part = -paired
         for r in range(0, rows, 128):
             at = slice(r, r + 128)
@@ -401,38 +404,56 @@
         ST[0, 8:] = part
         for c in stages[0]:
             c.start()
-    waiting = []
-    for lev in range(nd, -1, -1):
-        first, last = pos[levels[lev][0]], pos[levels[lev][-1]] + 1
-        low = 0 if lev == 1 else first
-        with jax.named_scope(f"texts{lev}"):
-            if lev:
-                weigh(0, last * ROWS, low, last)
+
+    spans = [(pos[ms[0]], pos[ms[-1]] + 1) for ms in levels]
+    with jax.named_scope("farthest"):
+        m = levels[nd][0]
+        weigh(0, rows, pos[m], nb)
+        text_grad(m)
+        spread_scalars()
+        weigh(pos[m] * ROWS, rows, 0, pos[m])
+        image_grad(pos[m], nb)
+        ready(m, imsg)
+        waiting = [m]
+    for lev in range(nd - 1, 1, -1):
+        with jax.named_scope(f"middle{lev}"):
+            first, last = spans[lev]
+            weigh(0, last * ROWS, first, last)
             for m in levels[lev]:
                 text_grad(m)
-                for w in waiting:
-                    pair(w)
-                waiting = []
-        if lev == 1:
-            with jax.named_scope("stats"):
-                ST[nb] = stat(0, stages[0])
-                for c in stages[1]:
-                    c.start()
-        with jax.named_scope(f"images{lev}"):
-            if lev > 1:
-                weigh(first * ROWS, last * ROWS, 0, first)
+                if len(waiting) > 1 or waiting[0] == levels[nd][0]:
+                    pair(waiting.pop(0))
+                at = pos[m]
+                weigh(at * ROWS, (at + 1) * ROWS, 0, first)
+                image_grad(at, at + 1)
+                ready(m, imsg)
+                waiting.append(m)
+            while waiting:
+                pair(waiting.pop(0))
+    with jax.named_scope("near"):
+        first, last = spans[1] if nd > 1 else (1, 1)
+        weigh(0, last * ROWS, 0, last)
+        for m in levels[1] if nd > 1 else []:
+            text_grad(m)
+    with jax.named_scope("stats"):
+        ST[nb] = stat(0, stages[0])
+        for c in stages[1]:
+            c.start()
+    with jax.named_scope("nearimages"):
+        while waiting:
+            pair(waiting.pop(0))
+        if nd > 1:
             image_grad(first, last)
-            if lev == 1 < nd:
-                follow(nd - 1, "i")
-            for m in levels[lev]:
+            follow(nd - 1, "i")
+            for m in levels[1]:
                 ready(m, imsg)
-            if lev == 1 < nd:
-                follow(nd - 1, "o")
-            if lev == nd:
-                waiting = list(levels[lev])
-            else:
-                for m in levels[lev]:
-                    pair(m)
+            follow(nd - 1, "o")
+        for m in levels[1] if nd > 1 else []:
+            pair(m)
+    with jax.named_scope("own"):
+        text_grad(0)
+        image_grad(0, 1)
+        pair(0)
     with jax.named_scope("follow"):
         for lev in range(nd - 2, 0, -1):
             follow(lev, "oi")
@@ -482,7 +503,7 @@
             vm((rows, width), bf16), vm((width, rows), bf16), vm((cols, width), bf16),
             vm((rows, cols), f32), vm((rows, cols), bf16),
             vm((rows, 128), f32), vm((rows, 128), f32), vm((rows, 128), f32), vm((rows, 128), f32),
-            vm((1, cols), f32), vm((1, cols), f32), vm((8, cols), f32), vm((8, cols), f32),
+            vm((8, cols), f32), vm((8, cols), f32), vm((8, cols), f32), vm((8, cols), f32),
             vm((nb, nb, 128), f32), vm((2 * nb, 2 * nb, 128), f32), vm((rows, 128), f32), vm((1, cols), f32),
             vm((rows, width), f32), vm((rows, width), f32),
             vm((2, nb, width, 128), f32), vm((nb, width, 128), f32), vm((nb, width, 128), f32),
@@ -496,7 +517,7 @@
             collective_id=0, has_side_effects=True, vmem_limit_bytes=60 * 2**20
         ),
         name="contrastive",
-    )(log_scale.reshape(1), images, texts)
+    )(log_scale, images, texts)
     outs = pl.pallas_call(
         hand_over,
         out_shape=(

time: 54.3 us -> 52.4 us (0.965)
  Pallas kernels: 52.9 us -> 50.9 us
    pallas_call x1, Pallas kernels: 51.2 us -> 49.3 us  [body(): pl.pallas_call(functools.partial(kernel, dims, total), out_shape=(jax.Sha...]
where the time goes in v6:
time: 52.4 us; the launch traced here: 52.2 us
  Pallas kernels  50.9 us (97%)
  between operations  1.29 us (2%)
    pallas_call x1, Pallas kernels, body(): pl.pallas_call(functools.partial(kernel, dims, total), out_shape=(jax.Sha...  49.3 us
    pallas_call x1, Pallas kernels, body(): pl.pallas_call(hand_over, out_shape=(jax.ShapeDtypeStruct(images.shape, b...  1.68 us

profile of v6, /device:TPU:1, one launch (start us, length us, event | category | flops | bytes accessed | tf_op | source)
XLA Modules:
  0.0 52.2 jit_solution(12784958598817996887)
XLA Ops:
  1.3 49.3 %contrastive.1 = (bf16[128,512]{1,0:T(8,128)(2,1)}, bf16[128,512]{1,0:T(8,128)(2,1)}, f32[8,128]{1,0:T(8,128)}) custom-call(f32[]{:T(128)S(6)} %copy.7.log_scale, bf16[128,512]{1,0:T(8,128)(2,1)} %images.1, bf16[128,512]{1,0:T(8,128)(2,1)} %texts.1), custom_call_target="tpu_custom_call" | custom-call | tf_op jit(solution)/shard_map/contrastive/pallas_call | solution.py:489
  50.5 1.7 %outputs.1 = (bf16[128,512]{1,0:T(8,128)(2,1)}, bf16[128,512]{1,0:T(8,128)(2,1)}, f32[1,1]{1,0:T(1,128)}, f32[1,1]{1,0:T(1,128)}) custom-call(bf16[128,512]{1,0:T(8,128)(2,1)} %get-tuple-element.11.gi, bf16[128,512]{1,0:T(8,128)(2,1)} %get-tuple-element.12.gt, f32[8,128]{1,0:T(8,128)} %get-tuple-element.13.stats), custom_call_target="tpu_custom_call" | custom-call | tf_op jit(solution)/shard_map/outputs/pallas_call | solution.py:521

commit v7 on v6

--- a/solution.py
+++ b/solution.py
@@ -130,18 +130,18 @@
         return send(T.at[pl.ds(at, n)], T.at[pl.ds(at + ROWS, n)], ds.at[m, p], dr.at[m, p], peer(0, "B", True))
 
     def pass_on(events):
-        for m, p in events:
-            xmsg(m, p).wait_recv()
         nxt = [(c, p) for m, p in events for c in cube.children(p, m)]
         nxt.sort(key=lambda e: not cube.children(e[1], e[0]))
-        for e in nxt:
-            go(xmsg(*e))
         for m, p in events:
             tmsg(m, p).wait_recv()
         for e in nxt:
             go(tmsg(*e))
         for e in events:
             go(dmsg(*e))
+        for m, p in events:
+            xmsg(m, p).wait_recv()
+        for e in nxt:
+            go(xmsg(*e))
 
     def logits(r0, r1, c0, c1):
         for i in range(c0, c1):
@@ -459,15 +459,16 @@
             follow(lev, "oi")
     with jax.named_scope("last"):
         for p in cube.pieces:
-            oadd(0, p)
-        gt_out[...] = (PT[0, 0] * scale).T.astype(jnp.bfloat16)
-        for p in cube.pieces:
             iadd(0, p)
         gi_out[...] = (PI[:128, :] * scale[:, :1]).astype(jnp.bfloat16)
         tile = stat(nb, stages[1])
         loss = jnp.sum(tile[:8]) * (LN2 * 0.5 / total)
         grad_scale = jnp.sum(tile[8:]) * (LN2 / total)
         stats_out[...] = jnp.where(line == 0, loss, grad_scale)
+    with jax.named_scope("lasttexts"):
+        for p in cube.pieces:
+            oadd(0, p)
+        gt_out[...] = (PT[0, 0] * scale).T.astype(jnp.bfloat16)
         for c in going + list(pmsg.values()) + stages[0] + stages[1]:
             c.wait_send()
 

time: 52.4 us -> 52.5 us (level)
  no operation moved by 1% of the time
where the time goes in v7:
time: 52.5 us; the launch traced here: 52.4 us
  Pallas kernels  51.1 us (97%)
  between operations  1.29 us (2%)
    pallas_call x1, Pallas kernels, body(): pl.pallas_call(functools.partial(kernel, dims, total), out_shape=(jax.Sha...  49.4 us
    pallas_call x1, Pallas kernels, body(): pl.pallas_call(hand_over, out_shape=(jax.ShapeDtypeStruct(images.shape, b...  1.68 us

profile of v7, /device:TPU:1, one launch (start us, length us, event | category | flops | bytes accessed | tf_op | source)
XLA Modules:
  0.0 52.4 jit_solution(13735510614148106922)
XLA Ops:
  1.3 49.4 %contrastive.1 = (bf16[128,512]{1,0:T(8,128)(2,1)}, bf16[128,512]{1,0:T(8,128)(2,1)}, f32[8,128]{1,0:T(8,128)}) custom-call(f32[]{:T(128)S(6)} %copy.7.log_scale, bf16[128,512]{1,0:T(8,128)(2,1)} %images.1, bf16[128,512]{1,0:T(8,128)(2,1)} %texts.1), custom_call_target="tpu_custom_call" | custom-call | tf_op jit(solution)/shard_map/contrastive/pallas_call | solution.py:490
  50.7 1.7 %outputs.1 = (bf16[128,512]{1,0:T(8,128)(2,1)}, bf16[128,512]{1,0:T(8,128)(2,1)}, f32[1,1]{1,0:T(1,128)}, f32[1,1]{1,0:T(1,128)}) custom-call(bf16[128,512]{1,0:T(8,128)(2,1)} %get-tuple-element.11.gi, bf16[128,512]{1,0:T(8,128)(2,1)} %get-tuple-element.12.gt, f32[8,128]{1,0:T(8,128)} %get-tuple-element.13.stats), custom_call_target="tpu_custom_call" | custom-call | tf_op jit(solution)/shard_map/outputs/pallas_call | solution.py:522

commit v8 on v7

--- a/solution.py
+++ b/solution.py
@@ -435,10 +435,6 @@
         weigh(0, last * ROWS, 0, last)
         for m in levels[1] if nd > 1 else []:
             text_grad(m)
-    with jax.named_scope("stats"):
-        ST[nb] = stat(0, stages[0])
-        for c in stages[1]:
-            c.start()
     with jax.named_scope("nearimages"):
         while waiting:
             pair(waiting.pop(0))
@@ -450,10 +446,13 @@
             follow(nd - 1, "o")
         for m in levels[1] if nd > 1 else []:
             pair(m)
+    with jax.named_scope("stats"):
+        ST[nb] = stat(0, stages[0])
+        for c in stages[1]:
+            c.start()
     with jax.named_scope("own"):
         text_grad(0)
         image_grad(0, 1)
-        pair(0)
     with jax.named_scope("follow"):
         for lev in range(nd - 2, 0, -1):
             follow(lev, "oi")
@@ -466,6 +465,7 @@
         grad_scale = jnp.sum(tile[8:]) * (LN2 / total)
         stats_out[...] = jnp.where(line == 0, loss, grad_scale)
     with jax.named_scope("lasttexts"):
+        pair(0)
         for p in cube.pieces:
             oadd(0, p)
         gt_out[...] = (PT[0, 0] * scale).T.astype(jnp.bfloat16)

time: 52.5 us -> 52.5 us (level)
  no operation moved by 1% of the time
where the time goes in v8:
time: 52.5 us; the launch traced here: 52.3 us
  Pallas kernels  51 us (97%)
  between operations  1.29 us (2%)
    pallas_call x1, Pallas kernels, body(): pl.pallas_call(functools.partial(kernel, dims, total), out_shape=(jax.Sha...  49.3 us
    pallas_call x1, Pallas kernels, body(): pl.pallas_call(hand_over, out_shape=(jax.ShapeDtypeStruct(images.shape, b...  1.68 us

profile of v8, /device:TPU:1, one launch (start us, length us, event | category | flops | bytes accessed | tf_op | source)
XLA Modules:
  0.0 52.3 jit_solution(13786996264537687353)
XLA Ops:
  1.3 49.3 %contrastive.1 = (bf16[128,512]{1,0:T(8,128)(2,1)}, bf16[128,512]{1,0:T(8,128)(2,1)}, f32[8,128]{1,0:T(8,128)}) custom-call(f32[]{:T(128)S(6)} %copy.7.log_scale, bf16[128,512]{1,0:T(8,128)(2,1)} %images.1, bf16[128,512]{1,0:T(8,128)(2,1)} %texts.1), custom_call_target="tpu_custom_call" | custom-call | tf_op jit(solution)/shard_map/contrastive/pallas_call | solution.py:490
  50.6 1.7 %outputs.1 = (bf16[128,512]{1,0:T(8,128)(2,1)}, bf16[128,512]{1,0:T(8,128)(2,1)}, f32[1,1]{1,0:T(1,128)}, f32[1,1]{1,0:T(1,128)}) custom-call(bf16[128,512]{1,0:T(8,128)(2,1)} %get-tuple-element.11.gi, bf16[128,512]{1,0:T(8,128)(2,1)} %get-tuple-element.12.gt, f32[8,128]{1,0:T(8,128)} %get-tuple-element.13.stats), custom_call_target="tpu_custom_call" | custom-call | tf_op jit(solution)/shard_map/outputs/pallas_call | solution.py:522

commit v9 on v8

--- a/solution.py
+++ b/solution.py
@@ -225,6 +225,15 @@
             sums(0, new, before, done)
 
     with jax.named_scope("lse"):
+        for m in order:
+            at = slice(pos[m] * 128, (pos[m] + 1) * 128)
+            tops = RM[at, :].T
+            top = jnp.max(tops, axis=0, keepdims=True)
+            part = jnp.sum(RS[at, :].T * jnp.exp2(tops - top), axis=0, keepdims=True)
+            RL[0, pl.ds(spot(m, "A"), 1), :] = top + jnp.log2(part)
+        rc = [send(RL.at[0], RL.at[m], rls.at[m], rlr.at[m], peer(m, "A")) for m in reversed(order[1:])]
+        for c in rc:
+            c.start()
         ctop = jnp.max(CM[...], axis=0, keepdims=True)
         ccol = ctop + jnp.log2(jnp.sum(CS[...] * jnp.exp2(CM[...] - ctop), axis=0, keepdims=True))
         for m in order:
@@ -237,15 +246,6 @@
             for m in reversed(order) for f in range(2) if m or f
         ]
         for c in cc:
-            c.start()
-        for m in order:
-            at = slice(pos[m] * 128, (pos[m] + 1) * 128)
-            tops = RM[at, :].T
-            top = jnp.max(tops, axis=0, keepdims=True)
-            part = jnp.sum(RS[at, :].T * jnp.exp2(tops - top), axis=0, keepdims=True)
-            RL[0, pl.ds(spot(m, "A"), 1), :] = top + jnp.log2(part)
-        rc = [send(RL.at[0], RL.at[m], rls.at[m], rlr.at[m], peer(m, "A")) for m in reversed(order[1:])]
-        for c in rc:
             c.start()
     with jax.named_scope("turn"):
         def tilt(c, _):

time: 52.5 us -> 52.1 us (level)
  no operation moved by 1% of the time
where the time goes in v9:
time: 52.1 us; the launch traced here: 52 us
  Pallas kernels  50.7 us (97%)
  between operations  1.29 us (2%)
    pallas_call x1, Pallas kernels, body(): pl.pallas_call(functools.partial(kernel, dims, total), out_shape=(jax.Sha...  49 us
    pallas_call x1, Pallas kernels, body(): pl.pallas_call(hand_over, out_shape=(jax.ShapeDtypeStruct(images.shape, b...  1.68 us

profile of v9, /device:TPU:1, one launch (start us, length us, event | category | flops | bytes accessed | tf_op | source)
XLA Modules:
  0.0 52.0 jit_solution(16709235832126468331)
XLA Ops:
  1.3 49.0 %contrastive.1 = (bf16[128,512]{1,0:T(8,128)(2,1)}, bf16[128,512]{1,0:T(8,128)(2,1)}, f32[8,128]{1,0:T(8,128)}) custom-call(f32[]{:T(128)S(6)} %copy.7.log_scale, bf16[128,512]{1,0:T(8,128)(2,1)} %images.1, bf16[128,512]{1,0:T(8,128)(2,1)} %texts.1), custom_call_target="tpu_custom_call" | custom-call | tf_op jit(solution)/shard_map/contrastive/pallas_call | solution.py:490
  50.3 1.7 %outputs.1 = (bf16[128,512]{1,0:T(8,128)(2,1)}, bf16[128,512]{1,0:T(8,128)(2,1)}, f32[1,1]{1,0:T(1,128)}, f32[1,1]{1,0:T(1,128)}) custom-call(bf16[128,512]{1,0:T(8,128)(2,1)} %get-tuple-element.11.gi, bf16[128,512]{1,0:T(8,128)(2,1)} %get-tuple-element.12.gt, f32[8,128]{1,0:T(8,128)} %get-tuple-element.13.stats), custom_call_target="tpu_custom_call" | custom-call | tf_op jit(solution)/shard_map/outputs/pallas_call | solution.py:522
